TPU v7x, 128 devices: a whole 4x4x4 slice. The times are simulated.
128 devices in a mesh: emb: 8 (over x, core), seq: 16 (over z, y).
Axes of the slice: x: 4, y: 4, z: 4, core: 2. Of those that a mesh axis runs over, the one named last changes fastest.
Arguments:
- token_rows: int32 [8, 8192], P('emb', 'seq'), may hold values from 0 to 4607, as said below
- segment_ids: int32 [8, 8192], P('emb', 'seq'), may hold values from 0 to 3, never falling along the last dimension, each value on 1 to 4096 neighbouring positions
- requests: int32 [128, 128, 4], P(('emb', 'seq')), may hold values from 0 to 8191, as said below
- hot_table: bfloat16 [4096, 512], replicated, may hold values from -6 to 6
- cold_table: bfloat16 [1048576, 512], P(('emb', 'seq')), may hold values from -6 to 6
- input_weight: bfloat16 [512, 2048], replicated, may hold values from -0.75 to 0.75
- output_weight: bfloat16 [512, 512], replicated, may hold values from -0.25 to 0.25
- up_weight: bfloat16 [512, 2048], replicated, may hold values from -0.25 to 0.25
- down_weight: bfloat16 [2048, 512], replicated, may hold values from -0.125 to 0.125
Outputs:
- layer_output: bfloat16 [8, 8192, 512], P('emb', 'seq')
Inputs may be any that keep to these rules, and one draw needn't show every extreme that they name: `token_rows`: A value below 4096 names that row of hot_table. A value 4096 + o * 4 + k names slot k of the holding device's requests to owner o, and that slot is always a live one. Exactly 256 positions of each device name request slots. For each requesting device and owner the live requests fill slots 0 to c - 1, with c from 1 to 4; dead slots hold 0. Some owners, the same ones for all requesters, get all 4 slots live from every device, and every draw has at least one such owner. `segment_ids`: segment numbers never fall along a sequence.
All inputs are finite; a program needn't handle non-finite values.
Results may differ from a plain program's by a relative error of at most 0.0087.
Values may be sent and summed in bfloat16 or wider, within the bound.
A program may use at most 128 MiB of HBM per device.

v0:
```python
import math

import jax
import jax.numpy as jnp
from jax import lax
from jax.sharding import PartitionSpec as P

H = 16


epsilon = 1e-06


def in_order(pieces, dim):
    shape = list(pieces.shape[1:])
    shape[dim] *= pieces.shape[0]
    return jnp.moveaxis(pieces, 0, dim).reshape(shape)


def copy_for_each(value, axis):
    devices = lax.axis_size(axis)
    return lax.all_to_all(
        jnp.broadcast_to(value[None], (devices, *value.shape)), axis, 0, 0, tiled=True
    )


def collect(value, axis, dim):
    return in_order(copy_for_each(value, axis), dim)


def normalize(values):
    widened = values.astype(jnp.float32)
    return widened * lax.rsqrt(jnp.mean(widened * widened, axis=-1, keepdims=True) + epsilon)


def attend(queries, key_rows, value_rows, segments):
    length, groups, head_width = queries.shape
    block_rows = math.gcd(length, 2048)
    blocks = length // block_rows
    score_scale = 1.0 / math.sqrt(head_width)
    query_blocks = queries.reshape(blocks, block_rows, groups, head_width)
    key_blocks = key_rows.reshape(blocks, block_rows, groups, head_width)
    value_blocks = value_rows.reshape(blocks, block_rows, groups, head_width)
    segment_blocks = segments.reshape(blocks, block_rows)
    offsets = jnp.arange(block_rows, dtype=jnp.int32)

    def one_block(inputs):
        query_block, query_segments, position = inputs
        query_places = position * block_rows + offsets

        def add_keys(key_step, running):
            key_block = lax.dynamic_index_in_dim(key_blocks, key_step, 0, keepdims=False)
            value_block = lax.dynamic_index_in_dim(value_blocks, key_step, 0, keepdims=False)
            key_segments = lax.dynamic_index_in_dim(segment_blocks, key_step, 0, keepdims=False)
            key_places = key_step * block_rows + offsets
            scores = (
                jnp.einsum(
                    "qgc,kgc->gqk", query_block, key_block, preferred_element_type=jnp.float32
                )
                * score_scale
            )
            allowed = (key_places[None, :] <= query_places[:, None]) & (
                query_segments[:, None] == key_segments[None, :]
            )
            weights = jnp.where(allowed[None], jax.nn.silu(scores), 0.0).astype(jnp.bfloat16)
            return running + jnp.einsum(
                "gqk,kgc->qgc", weights, value_block, preferred_element_type=jnp.float32
            )

        running = lax.fori_loop(
            0, position + 1, add_keys, jnp.zeros((block_rows, groups, head_width), jnp.float32)
        )
        return running.astype(jnp.bfloat16)

    attended = lax.map(
        one_block, (query_blocks, segment_blocks, jnp.arange(blocks, dtype=jnp.int32))
    )
    return attended.reshape(length, groups, head_width)


def local(
    token_rows,
    segment_ids,
    requests,
    hot_table,
    cold_table,
    input_weight,
    output_weight,
    up_weight,
    down_weight,
):
    emb_devices = lax.axis_size("emb")
    seq_devices = lax.axis_size("seq")
    all_devices = emb_devices * seq_devices
    capacity = requests.shape[2]
    hot_count = hot_table.shape[0]
    model_width = hot_table.shape[1]
    tokens_here = token_rows.shape[1]
    head_groups = H // seq_devices
    head_width = model_width // H
    requested = requests[0]
    fetched = lax.all_to_all(
        cold_table[
            lax.all_to_all(requested, ("emb", "seq"), split_axis=0, concat_axis=0, tiled=True)
        ],
        ("emb", "seq"),
        split_axis=0,
        concat_axis=0,
        tiled=True,
    )
    fetched = fetched.reshape(all_devices * capacity, model_width)
    item_ids = token_rows[0]
    is_hot = item_ids < hot_count
    hot_rows = hot_table[jnp.where(is_hot, item_ids, 0)]
    cold_rows = fetched[jnp.where(is_hot, 0, item_ids - hot_count)]
    embedded = jnp.where(is_hot[:, None], hot_rows, cold_rows)
    normed_input = normalize(embedded).astype(jnp.bfloat16)
    grouped_weight = input_weight.reshape(model_width, seq_devices, head_groups, 4, head_width)
    segments = collect(segment_ids, "seq", 1)[0]
    gate_rounded = jnp.einsum(
        "td,dgec->gtec",
        normed_input,
        grouped_weight[:, :, :, 0, :],
        preferred_element_type=jnp.float32,
    ).astype(jnp.bfloat16)
    gate_units = jax.nn.silu(lax.optimization_barrier(gate_rounded).astype(jnp.float32))
    own_group = lax.axis_index("seq")
    own_weight = lax.dynamic_index_in_dim(grouped_weight, own_group, 1, keepdims=False)[
        :, :, 1:, :
    ].reshape(model_width, head_groups * 3 * head_width)
    gathered = jnp.dot(
        lax.all_gather(normed_input, "seq", axis=0, tiled=True),
        own_weight,
        preferred_element_type=jnp.float32,
    ).astype(jnp.bfloat16)
    head_rows = gathered.reshape(tokens_here * seq_devices, head_groups, 3, head_width)
    attended = attend(head_rows[:, :, 1], head_rows[:, :, 2], head_rows[:, :, 0], segments)
    returned = lax.all_to_all(
        attended.reshape(seq_devices, tokens_here * head_groups * head_width),
        "seq",
        split_axis=0,
        concat_axis=0,
        tiled=True,
    )
    returned = returned.reshape(seq_devices, tokens_here, head_groups, head_width).astype(
        jnp.float32
    )
    mean_square = jnp.mean(returned * returned, axis=(0, 2, 3))
    normed_heads = (
        returned * lax.rsqrt(mean_square + epsilon)[None, :, None, None] * gate_units
    ).astype(jnp.bfloat16)
    hidden = embedded.astype(jnp.float32) + jnp.einsum(
        "gtc,gcd->td",
        normed_heads.reshape(seq_devices, tokens_here, head_groups * head_width),
        output_weight.reshape(seq_devices, head_groups * head_width, model_width),
        preferred_element_type=jnp.float32,
    )
    normed_hidden = normalize(hidden).astype(jnp.bfloat16)
    activated = jax.nn.silu(
        jnp.dot(normed_hidden, up_weight, preferred_element_type=jnp.float32)
    ).astype(jnp.bfloat16)
    layer_output = (
        hidden + jnp.dot(activated, down_weight, preferred_element_type=jnp.float32)
    ).astype(jnp.bfloat16)
    return layer_output[None]


def solution(mesh):
    placed = (
        P("emb", "seq"),
        P("emb", "seq"),
        P(("emb", "seq"), None, None),
        P(),
        P(("emb", "seq"), None),
        P(),
        P(),
        P(),
        P(),
    )
    return jax.shard_map(
        local, mesh=mesh, in_specs=placed, out_specs=P("emb", "seq", None), check_vma=False
    )
```

profile of v0, /device:TPU:0, one launch (start us, length us, event | category | flops | bytes accessed | tf_op | source)
XLA Modules:
  0.0 304.7 jit_solution(13476258196587185154)
XLA Ops:
  7.5 20.5 %all_to_all.32 = s32[128,1,4]{2,1,0:T(1,128)S(1)} all-to-all(s32[128,1,4]{2,1,0:T(1,128)S(1)} %bitcast.141), channel_id=1, replica_groups=mesh['emb'=8,'seq'=16] {'emb','seq'}, dimensions={0} | all-to-all | bytes 4096 | tf_op jit(solution)/shard_map/all_to_all | solution.py:104
  28.1 6.4 %gather_fusion.1 = bf16[512,512]{1,0:T(8,128)(2,1)S(1)} fusion(bf16[8192,512]{1,0:T(8,128)(2,1)} %param.17, s32[1024]{0:T(1024)S(1)} %pad_clamp_fusion.1), kind=kCustom, calls=%fused_computation.1 | custom fusion | bytes 1050624 | tf_op jit(solution)/shard_map/gather | solution.py:103
  35.5 5.7 %all-to-all-start.1 = ((bf16[128,4,512]{2,1,0:T(4,128)(2,1)}), bf16[128,4,512]{2,1,0:T(4,128)(2,1)}, u32[]{:S(2)}, u32[]{:S(2)}) async-start(bf16[128,4,512]{2,1,0:T(4,128)(2,1)} %reshape.217), calls=%async_computation.1 | async-start | bytes 1048576 | tf_op jit(solution)/shard_map/all_to_all | solution.py:102
  41.3 4.7 %gather_fusion = bf16[512,512]{1,0:T(8,128)(2,1)S(1)} fusion(bf16[4096,512]{1,0:T(8,128)(2,1)} %param.16, s32[1024]{0:T(1024)S(1)} %pad_clamp_fusion.2), kind=kCustom, calls=%fused_computation | custom fusion | bytes 1050624 | tf_op jit(solution)/shard_map/gather | solution.py:114
  46.3 8.1 %all-to-all-done.1 = bf16[128,4,512]{2,1,0:T(4,128)(2,1)} async-done(((bf16[128,4,512]{2,1,0:T(4,128)(2,1)}), bf16[128,4,512]{2,1,0:T(4,128)(2,1)}, u32[]{:S(2)}, u32[]{:S(2)}) %all-to-all-start.1) | async-done | bytes 524320 | tf_op jit(solution)/shard_map/all_to_all | solution.py:102
  62.1 3.7 %all-to-all-start.2 = ((s32[16,1,512]{2,1,0:T(1,128)}), s32[16,1,512]{2,1,0:T(1,128)S(1)}, u32[]{:S(2)}, u32[]{:S(2)}) async-start(s32[16,1,512]{2,1,0:T(1,128)} %broadcast_in_dim.52), calls=%async_computation.2 | async-start | bytes 65536 | tf_op jit(solution)/shard_map/all_to_all | solution.py:22
  65.7 4.0 %copy.46 = bf16[512,2048]{0,1:T(8,128)(2,1)} copy(bf16[512,2048]{1,0:T(8,128)(2,1)} %param.18) | data formatting | bytes 4194304 | tf_op args[5]
  73.2 61.5 %all-gather.2.cloned.1.call-done = bf16[8192,512]{0,1:T(8,128)(2,1)} async-done(((bf16[512,512]{0,1:T(8,128)(2,1)}), bf16[8192,512]{0,1:T(8,128)(2,1)}) %all-gather.2.cloned.1.call-update) | async-done | bytes 8388624 | tf_op jit(solution)/shard_map/all_gather | solution.py:132
  134.7 4.8 %convolution_convert_fusion = bf16[8192,96]{0,1:T(8,128)(2,1)S(1)} fusion(bf16[512,96]{0,1:T(8,128)(2,1)S(1)} %bitcast.139, bf16[8192,512]{0,1:T(8,128)(2,1)} %all-gather.2.cloned.1.call-done), kind=kOutput, calls=%fused_computation.29 | convolution fusion | flops 806092800 | bytes 10059776 | tf_op jit(solution)/shard_map/dot_general | solution.py:131
  151.9 93.7 %while.25 = (s32[]{:T(128)}, bf16[4,2048,1,32]{1,3,2,0:T(8,128)(2,1)}, s32[4]{0:T(128)S(1)}, bf16[4,2048,1,32]{1,3,2,0:T(8,128)(2,1)S(1)}, s32[4,2048]{1,0:T(4,1...) while((s32[]{:T(128)}, ...), condition=%wide.region_4.5_spmd.clone.clone, body=%wide.region_1.4_spmd.clone.clone.sunk | while | flops 578949120 | bytes 1934864 | solution.py:75
  153.9 8.3 %while.26 = (s32[]{:T(128)}, f32[2048,1,32]{0,2,1:T(8,128)S(1)}, s32[]{:T(128)}, bf16[4,2048,1,32]{1,3,2,0:T(8,128)(2,1)}, s32[2048]{0:T(1024)S(1)}, /*index=5*/...) while((s32[]{:T(128)}, f32[2048,1,32]{0,2,1:T(8,128)S(1)}, ...), condition=%wide.region_3.3_spmd, body=%wide.region_2.2_spmd.sunk | while | flops 578881536 | bytes 984259 | solution.py:70
  154.0 8.2 %fusion.59 = f32[2048,1,32]{0,2,1:T(8,128)S(1)} fusion(f32[2048,1,32]{0,2,1:T(8,128)S(1)} %get-tuple-element.351, s32[2048]{0:T(1024)S(1)} %get-tuple-element.370, s32[2048]{0:T(1024)S(1)} %get-tuple-element.369, s32[2048]{0:T(1024)S(1)} %bitcast.134, s32[2048]{0:T(1024)S(1)} %broadcast_add_fusion.2, ...), kind=kOutput, calls=%fused_computation.13.clone.1 | convolution fusion | flops 578879488 | bytes 951296 | tf_op jit(solution)/shard_map/while/body/eval_jaxpr/while/body/gqk,kgc->qgc/dot_general | solution.py:66
  164.9 16.6 %while.26 = (s32[]{:T(128)}, f32[2048,1,32]{0,2,1:T(8,128)S(1)}, s32[]{:T(128)}, bf16[4,2048,1,32]{1,3,2,0:T(8,128)(2,1)}, s32[2048]{0:T(1024)S(1)}, /*index=5*/...) while((s32[]{:T(128)}, f32[2048,1,32]{0,2,1:T(8,128)S(1)}, ...), condition=%wide.region_3.3_spmd, body=%wide.region_2.2_spmd.sunk | while | flops 578881536 | bytes 984259 | solution.py:70
  164.9 8.3 %fusion.59 = f32[2048,1,32]{0,2,1:T(8,128)S(1)} fusion(f32[2048,1,32]{0,2,1:T(8,128)S(1)} %get-tuple-element.351, s32[2048]{0:T(1024)S(1)} %get-tuple-element.370, s32[2048]{0:T(1024)S(1)} %get-tuple-element.369, s32[2048]{0:T(1024)S(1)} %bitcast.134, s32[2048]{0:T(1024)S(1)} %broadcast_add_fusion.2, ...), kind=kOutput, calls=%fused_computation.13.clone.1 | convolution fusion | flops 578879488 | bytes 951296 | tf_op jit(solution)/shard_map/while/body/eval_jaxpr/while/body/gqk,kgc->qgc/dot_general | solution.py:66
  173.3 8.2 %fusion.59 = f32[2048,1,32]{0,2,1:T(8,128)S(1)} fusion(f32[2048,1,32]{0,2,1:T(8,128)S(1)} %get-tuple-element.351, s32[2048]{0:T(1024)S(1)} %get-tuple-element.370, s32[2048]{0:T(1024)S(1)} %get-tuple-element.369, s32[2048]{0:T(1024)S(1)} %bitcast.134, s32[2048]{0:T(1024)S(1)} %broadcast_add_fusion.2, ...), kind=kOutput, calls=%fused_computation.13.clone.1 | convolution fusion | flops 578879488 | bytes 951296 | tf_op jit(solution)/shard_map/while/body/eval_jaxpr/while/body/gqk,kgc->qgc/dot_general | solution.py:66
  184.2 24.9 %while.26 = (s32[]{:T(128)}, f32[2048,1,32]{0,2,1:T(8,128)S(1)}, s32[]{:T(128)}, bf16[4,2048,1,32]{1,3,2,0:T(8,128)(2,1)}, s32[2048]{0:T(1024)S(1)}, /*index=5*/...) while((s32[]{:T(128)}, f32[2048,1,32]{0,2,1:T(8,128)S(1)}, ...), condition=%wide.region_3.3_spmd, body=%wide.region_2.2_spmd.sunk | while | flops 578881536 | bytes 984259 | solution.py:70
  184.2 8.2 %fusion.59 = f32[2048,1,32]{0,2,1:T(8,128)S(1)} fusion(f32[2048,1,32]{0,2,1:T(8,128)S(1)} %get-tuple-element.351, s32[2048]{0:T(1024)S(1)} %get-tuple-element.370, s32[2048]{0:T(1024)S(1)} %get-tuple-element.369, s32[2048]{0:T(1024)S(1)} %bitcast.134, s32[2048]{0:T(1024)S(1)} %broadcast_add_fusion.2, ...), kind=kOutput, calls=%fused_computation.13.clone.1 | convolution fusion | flops 578879488 | bytes 951296 | tf_op jit(solution)/shard_map/while/body/eval_jaxpr/while/body/gqk,kgc->qgc/dot_general | solution.py:66
  192.5 8.2 %fusion.59 = f32[2048,1,32]{0,2,1:T(8,128)S(1)} fusion(f32[2048,1,32]{0,2,1:T(8,128)S(1)} %get-tuple-element.351, s32[2048]{0:T(1024)S(1)} %get-tuple-element.370, s32[2048]{0:T(1024)S(1)} %get-tuple-element.369, s32[2048]{0:T(1024)S(1)} %bitcast.134, s32[2048]{0:T(1024)S(1)} %broadcast_add_fusion.2, ...), kind=kOutput, calls=%fused_computation.13.clone.1 | convolution fusion | flops 578879488 | bytes 951296 | tf_op jit(solution)/shard_map/while/body/eval_jaxpr/while/body/gqk,kgc->qgc/dot_general | solution.py:66
  200.8 8.2 %fusion.59 = f32[2048,1,32]{0,2,1:T(8,128)S(1)} fusion(f32[2048,1,32]{0,2,1:T(8,128)S(1)} %get-tuple-element.351, s32[2048]{0:T(1024)S(1)} %get-tuple-element.370, s32[2048]{0:T(1024)S(1)} %get-tuple-element.369, s32[2048]{0:T(1024)S(1)} %bitcast.134, s32[2048]{0:T(1024)S(1)} %broadcast_add_fusion.2, ...), kind=kOutput, calls=%fused_computation.13.clone.1 | convolution fusion | flops 578879488 | bytes 951296 | tf_op jit(solution)/shard_map/while/body/eval_jaxpr/while/body/gqk,kgc->qgc/dot_general | solution.py:66
  211.7 33.2 %while.26 = (s32[]{:T(128)}, f32[2048,1,32]{0,2,1:T(8,128)S(1)}, s32[]{:T(128)}, bf16[4,2048,1,32]{1,3,2,0:T(8,128)(2,1)}, s32[2048]{0:T(1024)S(1)}, /*index=5*/...) while((s32[]{:T(128)}, f32[2048,1,32]{0,2,1:T(8,128)S(1)}, ...), condition=%wide.region_3.3_spmd, body=%wide.region_2.2_spmd.sunk | while | flops 578881536 | bytes 984259 | solution.py:70
  211.8 8.2 %fusion.59 = f32[2048,1,32]{0,2,1:T(8,128)S(1)} fusion(f32[2048,1,32]{0,2,1:T(8,128)S(1)} %get-tuple-element.351, s32[2048]{0:T(1024)S(1)} %get-tuple-element.370, s32[2048]{0:T(1024)S(1)} %get-tuple-element.369, s32[2048]{0:T(1024)S(1)} %bitcast.134, s32[2048]{0:T(1024)S(1)} %broadcast_add_fusion.2, ...), kind=kOutput, calls=%fused_computation.13.clone.1 | convolution fusion | flops 578879488 | bytes 951296 | tf_op jit(solution)/shard_map/while/body/eval_jaxpr/while/body/gqk,kgc->qgc/dot_general | solution.py:66
  220.1 8.2 %fusion.59 = f32[2048,1,32]{0,2,1:T(8,128)S(1)} fusion(f32[2048,1,32]{0,2,1:T(8,128)S(1)} %get-tuple-element.351, s32[2048]{0:T(1024)S(1)} %get-tuple-element.370, s32[2048]{0:T(1024)S(1)} %get-tuple-element.369, s32[2048]{0:T(1024)S(1)} %bitcast.134, s32[2048]{0:T(1024)S(1)} %broadcast_add_fusion.2, ...), kind=kOutput, calls=%fused_computation.13.clone.1 | convolution fusion | flops 578879488 | bytes 951296 | tf_op jit(solution)/shard_map/while/body/eval_jaxpr/while/body/gqk,kgc->qgc/dot_general | solution.py:66
  228.4 8.2 %fusion.59 = f32[2048,1,32]{0,2,1:T(8,128)S(1)} fusion(f32[2048,1,32]{0,2,1:T(8,128)S(1)} %get-tuple-element.351, s32[2048]{0:T(1024)S(1)} %get-tuple-element.370, s32[2048]{0:T(1024)S(1)} %get-tuple-element.369, s32[2048]{0:T(1024)S(1)} %bitcast.134, s32[2048]{0:T(1024)S(1)} %broadcast_add_fusion.2, ...), kind=kOutput, calls=%fused_computation.13.clone.1 | convolution fusion | flops 578879488 | bytes 951296 | tf_op jit(solution)/shard_map/while/body/eval_jaxpr/while/body/gqk,kgc->qgc/dot_general | solution.py:66
  236.7 8.2 %fusion.59 = f32[2048,1,32]{0,2,1:T(8,128)S(1)} fusion(f32[2048,1,32]{0,2,1:T(8,128)S(1)} %get-tuple-element.351, s32[2048]{0:T(1024)S(1)} %get-tuple-element.370, s32[2048]{0:T(1024)S(1)} %get-tuple-element.369, s32[2048]{0:T(1024)S(1)} %bitcast.134, s32[2048]{0:T(1024)S(1)} %broadcast_add_fusion.2, ...), kind=kOutput, calls=%fused_computation.13.clone.1 | convolution fusion | flops 578879488 | bytes 951296 | tf_op jit(solution)/shard_map/while/body/eval_jaxpr/while/body/gqk,kgc->qgc/dot_general | solution.py:66
  248.4 5.4 %all_to_all.27 = bf16[16,1,16384]{2,1,0:T(2,128)(2,1)} reshape(bf16[4,2048,1,32]{3,1,0,2:T(8,128)(2,1)} %copy.50) | data formatting | bytes 1048576 | tf_op jit(solution)/shard_map/all_to_all | solution.py:138
  254.4 5.0 %reduce.9 = bf16[16,16384]{1,0:T(8,128)(2,1)S(1)} reduce(bf16[16,1,16384]{2,1,0:T(2,128)(2,1)} %all_to_all.27, bf16[]{:T(256)} %broadcast.198), dimensions={1}, to_apply=%all_to_all.27.reduce_sub_computation | reduce | bytes 1048578 | tf_op jit(solution)/shard_map/all_to_all | solution.py:138
  260.5 4.9 %all-to-all-start.3 = ((bf16[16,2,8192]{2,1,0:T(2,128)(2,1)}), bf16[16,2,8192]{2,1,0:T(2,128)(2,1)S(1)}, u32[]{:S(2)}, u32[]{:S(2)}) async-start(bf16[16,2,8192]{2,1,0:T(2,128)(2,1)} %reshape.239), calls=%async_computation.3 | async-start | bytes 1048576 | tf_op jit(solution)/shard_map/all_to_all | solution.py:138
  267.9 7.9 %all-to-all-done.3 = bf16[16,2,8192]{2,1,0:T(2,128)(2,1)S(1)} async-done(((bf16[16,2,8192]{2,1,0:T(2,128)(2,1)}), bf16[16,2,8192]{2,1,0:T(2,128)(2,1)S(1)}, u32[]{:S(2)}, u32[]{:S(2)}) %all-to-all-start.3) | async-done | bytes 524320 | tf_op jit(solution)/shard_map/all_to_all | solution.py:138
  277.5 4.7 %fusion.33 = (f32[16384]{0:T(1024)S(1)}, f32[16,16384]{1,0:T(8,128)S(1)}) fusion(bf16[16,1,16384]{2,1,0:T(2,128)(2,1)} %reshape.240), kind=kLoop, calls=%fused_computation.49 | loop fusion | flops 770048 | bytes 1638400 | tf_op jit(solution)/shard_map/reduce_sum | solution.py:148
  284.9 3.7 %copy.52 = f32[16,512,1,32]{1,3,0,2:T(8,128)} copy(f32[16,512,1,32]{3,1,0,2:T(8,128)} %reshape.207) | data formatting | bytes 2097152 | tf_op jit(solution)/shard_map/convert_element_type | solution.py:145
  288.9 3.0 multiply_reduce_fusion
  291.9 5.0 %fusion.26 = bf16[1,512,512]{1,2,0:T(8,128)(2,1)S(1)} fusion(f32[512,512]{0,1:T(8,128)} %get-tuple-element.207, bf16[2048,512]{1,0:T(8,128)(2,1)S(1)} %copy-done, bf16[512,2048]{1,0:T(8,128)(2,1)} %param.20, f32[512]{0:T(512)S(1)} %add_rsqrt_fusion), kind=kOutput, calls=%fused_computation.40 | convolution fusion | flops 2153775104 | bytes 5769216 | tf_op jit(solution)/shard_map/dot_general | solution.py:163
  (108 shorter events, 43.8 us)
Async XLA Ops:
  6.5 285.4 %copy-start = (bf16[2048,512]{1,0:T(8,128)(2,1)S(1)}, bf16[2048,512]{1,0:T(8,128)(2,1)}, u32[]{:S(2)}) copy-start(bf16[2048,512]{1,0:T(8,128)(2,1)} %param.21) | copy-start | bytes 6291460
  6.5 34.7 %copy-start.5 = (s32[1,512]{1,0:T(1,128)S(1)}, s32[1,512]{1,0:T(1,128)}, u32[]{:S(2)}) copy-start(s32[1,512]{1,0:T(1,128)} %param.13) | copy-start | bytes 6148
  35.5 18.9 %all-to-all-start.1 = ((bf16[128,4,512]{2,1,0:T(4,128)(2,1)}), bf16[128,4,512]{2,1,0:T(4,128)(2,1)}, u32[]{:S(2)}, u32[]{:S(2)}) async-start(bf16[128,4,512]{2,1,0:T(4,128)(2,1)} %reshape.217), calls=%async_computation.1 | async-start | bytes 1048576 | tf_op jit(solution)/shard_map/all_to_all | solution.py:102
  41.2 93.5 %all-gather.2.cloned.1.call-start = ((), (), s32[]{:S(2)}) async-start(), calls=%async_computation.4 | async-start | bytes 8912896 | tf_op jit(solution)/shard_map/all_gather | solution.py:132
  55.6 5.9 %copy-start.6 = (s32[1,512]{1,0:T(1,128)S(1)}, s32[1,512]{1,0:T(1,128)}, u32[]{:S(2)}) copy-start(s32[1,512]{1,0:T(1,128)} %param.14) | copy-start | bytes 6148
  59.7 0.8 copy-start.2
  62.1 11.0 %all-to-all-start.2 = ((s32[16,1,512]{2,1,0:T(1,128)}), s32[16,1,512]{2,1,0:T(1,128)S(1)}, u32[]{:S(2)}, u32[]{:S(2)}) async-start(s32[16,1,512]{2,1,0:T(1,128)} %broadcast_in_dim.52), calls=%async_computation.2 | async-start | bytes 65536 | tf_op jit(solution)/shard_map/all_to_all | solution.py:22
  245.6 19.9 %copy-start.1 = (bf16[512,512]{0,1:T(8,128)(2,1)S(1)}, bf16[512,512]{0,1:T(8,128)(2,1)}, u32[]{:S(2)}) copy-start(bf16[512,512]{0,1:T(8,128)(2,1)} %fusion.32) | copy-start | bytes 1572868
  260.5 15.2 %all-to-all-start.3 = ((bf16[16,2,8192]{2,1,0:T(2,128)(2,1)}), bf16[16,2,8192]{2,1,0:T(2,128)(2,1)S(1)}, u32[]{:S(2)}, u32[]{:S(2)}) async-start(bf16[16,2,8192]{2,1,0:T(2,128)(2,1)} %reshape.239), calls=%async_computation.3 | async-start | bytes 1048576 | tf_op jit(solution)/shard_map/all_to_all | solution.py:138
  284.9 4.0 %copy-start.3 = (bf16[512,512]{0,1:T(8,128)(2,1)S(1)}, bf16[512,512]{0,1:T(8,128)(2,1)}, u32[]{:S(2)}) copy-start(bf16[512,512]{0,1:T(8,128)(2,1)} %copy-done.2) | copy-start | bytes 1572868
  284.9 4.0 %copy-start.4 = (bf16[16,512,1,32]{1,3,0,2:T(8,128)(2,1)S(1)}, bf16[16,512,1,32]{1,3,0,2:T(8,128)(2,1)}, u32[]{:S(2)}) copy-start(bf16[16,512,1,32]{1,3,0,2:T(8,128)(2,1)} %convert_bitcast_fusion) | copy-start | bytes 1572868
Sparse Core Ops, SparseCore 0:
  61.5 73.1 all-gather.1
where the time goes:
time: 306 us; the launch traced here: 305 us
  matrix products  96.7 us (32%)
  waiting for transfers between devices  78 us (25%)
  local copies, waits for them, and re-layouts  61.1 us (20%)
  blocking collectives  20.5 us (7%)
  other arithmetic  14.7 us (5%)
  starting transfers between devices  14.4 us (5%)
  between operations  13.6 us (4%)
  loops' own time  5.8 us (2%)
    dot_general x10, matrix products, add_keys(): jnp.einsum('gqk,kgc->qgc', weights, value_block, preferred_element_type=j...  82.4 us
    all_gather x1, waiting for transfers between devices, local(): lax.all_gather(normed_input, 'seq', axis=0, tiled=True)  61.5 us
    all_to_all x1, blocking collectives, local(): lax.all_to_all(requested, ('emb', 'seq'), split_axis=0, concat_axis=0, ti...  20.5 us
    unnamed x21, local copies, waits for them, and re-layouts  14.4 us
    all_to_all x1, waiting for transfers between devices, local(): lax.all_to_all(cold_table[lax.all_to_all(requested, ('emb', 'seq'), split...  8.09 us
    all_to_all x1, waiting for transfers between devices, local(): lax.all_to_all(attended.reshape(seq_devices, tokens_here * head_groups *...  7.86 us
    gather x2, local copies, waits for them, and re-layouts, local(): cold_table[lax.all_to_all(requested, ('emb', 'seq'), split_axis=0, concat...  7.36 us
    convert_element_type x2, local copies, waits for them, and re-layouts, local(): returned.reshape(seq_devices, tokens_here, head_groups, head_width)  6.41 us
  transfers between devices with their start and end apart: 4, of which 4 were waited for; matrix products, arithmetic and copies ran while one was open for 5% of the time, Pallas kernels for 0%

commit v1 on v0

v1 whole, which is shorter than its diff:
```python
import functools
import math

import jax
import jax.numpy as jnp
from jax import lax
from jax.experimental import pallas as pl
from jax.experimental.pallas import tpu as pltpu
from jax.sharding import PartitionSpec as P

H = 16
epsilon = 1e-06

BIG = float(2 ** 30)

def attn_kernel(TQ, TK, U, BF, starts_ref, qkv_ref, out_ref, q_scr, k_scr, v_scr, m_scr, a_scr, acc_scr):
    nb, _, W = qkv_ref.shape
    L = nb * W
    NQ = L // TQ
    s1, s2, s3 = starts_ref[0], starts_ref[1], starts_ref[2]
    C = 0.5 / (32.0 ** 0.5)
    bf = jnp.bfloat16

    def prep(b, _):
        base = b * W
        lane = lax.broadcasted_iota(jnp.int32, (16, W), 1) + base
        row = lax.broadcasted_iota(jnp.int32, (16, W), 0)
        seg = (lane >= s1).astype(jnp.int32) + (lane >= s2).astype(jnp.int32) + (lane >= s3).astype(jnp.int32)
        hot = (seg == row).astype(jnp.float32)
        q = qkv_ref[b, 32:64, :].astype(jnp.float32) * C
        qx = jnp.concatenate([q.astype(bf), hot.astype(bf)], axis=0)
        for c in range(W // 256):
            q_scr[b * (W // 256) + c] = qx[:, c * 256:(c + 1) * 256]
        bias = jnp.where(row < 4, (1.0 - hot) * (-BIG), 0.0)
        kx = jnp.concatenate([qkv_ref[b, 64:96, :].astype(jnp.float32), bias], axis=0)
        k_scr[pl.ds(base, W), :] = kx.T.astype(bf)
        v = qkv_ref[b, 0:32, :]
        for c in range(W // 256):
            v_scr[b * (W // 256) + c] = v[:, c * 256:(c + 1) * 256]
        return 0
    lax.fori_loop(0, nb, prep, 0)

    R = TQ // TK
    for r in range(R):
        t = lax.broadcasted_iota(jnp.int32, (TK, TQ), 0) + r * TK
        qq = lax.broadcasted_iota(jnp.int32, (TK, TQ), 1)
        m_scr[r] = (t <= qq).astype(jnp.float32).astype(bf)
    m_scr[R] = jnp.ones((TK, TQ), bf)
    m_scr[R + 1] = jnp.zeros((TK, TQ), bf)

    def lo_of(i):
        p0 = i * TQ
        st = jnp.where(p0 >= s3, s3, jnp.where(p0 >= s2, s2, jnp.where(p0 >= s1, s1, 0)))
        return st // TK

    def count(i, n):
        return n + (i * R + R - lo_of(i))
    total = lax.fori_loop(0, NQ, count, 0)
    steps = (total + U - 1) // U

    def nxt(i, j):
        last = j <= lo_of(i)
        i2 = jnp.where(last, i + 1, i)
        j2 = jnp.where(last, (i + 1) * R + R - 1, j - 1)
        return i2, j2

    qh = TQ // 256
    kh = TK // 256

    def make(slot, i, j, valid):
        d = j - i * R
        ms = jnp.where(valid, jnp.where(d >= 0, d, R), R + 1)
        k = k_scr[pl.ds(j * TK, TK), :]
        for c in range(qh):
            q = q_scr[i * qh + c]
            s = jnp.dot(k, q, preferred_element_type=jnp.float32)
            if BF:
                h = s.astype(bf)
                a = h + h * jnp.tanh(h)
            else:
                a = (s + s * jnp.tanh(s)).astype(bf)
            a = a * m_scr[ms, :, c * 256:(c + 1) * 256]
            a_scr[slot, :, c * 256:(c + 1) * 256] = a

    def consume(slot, i, j, valid):
        first = j == i * R + R - 1
        for c in range(qh):
            o = jnp.where(first, 0.0, acc_scr[:, c * 256:(c + 1) * 256])
            for t in range(kh):
                o = o + jnp.dot(v_scr[j * kh + t], a_scr[slot, t * 256:(t + 1) * 256, c * 256:(c + 1) * 256],
                                preferred_element_type=jnp.float32)
            acc_scr[:, c * 256:(c + 1) * 256] = o
            if TQ <= W:
                bi = i // (W // TQ)
                if W == TQ:
                    out_ref[bi, :, c * 256:(c + 1) * 256] = o.astype(bf)
                else:
                    off = pl.multiple_of((i % (W // TQ)) * TQ, 256)
                    out_ref[bi, :, pl.ds(off, 256)] = o.astype(bf)
            else:
                out_ref[i * (TQ // W) + (c * 256) // W, :, (c * 256) % W:(c * 256) % W + 256] = o.astype(bf)

    def seq(n0, i, j):
        out = []
        for u in range(U):
            valid = n0 + u < total
            ic = jnp.where(valid, i, 0)
            jc = jnp.where(valid, j, 0)
            out.append((i, j, valid))
            i, j = nxt(i, j)
        return out, i, j

    def clamp(i, j, valid):
        return jnp.minimum(i, NQ - 1), jnp.where(valid, j, 0)

    i0 = jnp.int32(0); j0 = jnp.int32(R - 1)
    lst, i1, j1 = seq(0, i0, j0)
    for u, (i, j, v) in enumerate(lst):
        ci, cj = clamp(i, j, v)
        make(u, ci, cj, v)

    def body(n, carry):
        i, j, ni, nj = carry
        lst, _, _ = seq(n * U, i, j)
        lst2, n2i, n2j = seq((n + 1) * U, ni, nj)
        for u in range(U):
            ci, cj = clamp(*lst[u])
            consume(u, ci, cj, lst[u][2])
        for u in range(U):
            ci, cj = clamp(*lst2[u])
            make(u, ci, cj, lst2[u][2])
        return (ni, nj, n2i, n2j)
    lax.fori_loop(0, steps, body, (i0, j0, i1, j1))


def attention(starts, qkv, TQ=512, TK=512, U=1, BF=True):
    nb, _, W = qkv.shape
    L = nb * W
    bf = jnp.bfloat16
    R = TQ // TK
    return pl.pallas_call(
        functools.partial(attn_kernel, TQ, TK, U, BF),
        out_shape=jax.ShapeDtypeStruct((nb, 32, W), bf),
        in_specs=[pl.BlockSpec(memory_space=pltpu.SMEM), pl.BlockSpec(memory_space=pltpu.VMEM)],
        out_specs=pl.BlockSpec(memory_space=pltpu.VMEM),
        scratch_shapes=[
            pltpu.VMEM((L // 256, 48, 256), bf),
            pltpu.VMEM((L, 48), bf),
            pltpu.VMEM((L // 256, 32, 256), bf),
            pltpu.VMEM((R + 2, TK, TQ), bf),
            pltpu.VMEM((U, TK, TQ), bf),
            pltpu.VMEM((32, TQ), jnp.float32),
        ],
        compiler_params=pltpu.CompilerParams(vmem_limit_bytes=60 << 20),
        name="attn",
    )(starts, qkv)


MESH = pl.DeviceIdType.MESH


def greet(axis_size):
    me = lax.axis_index("seq")
    barrier = pltpu.get_barrier_semaphore()

    def signal(step, carry):
        peer = lax.rem(me + step, axis_size)
        pl.semaphore_signal(barrier, inc=1, device_id={"seq": peer}, device_id_type=MESH)
        return carry

    lax.fori_loop(1, axis_size, signal, 0)
    pl.semaphore_wait(barrier, axis_size - 1)


def project_kernel(n, emb_ref, w_hbm, count_ref, gate_ref, recv_ref, counts_ref, w_ref, x_ref, send, sends, recvs, csends, crecvs, wsem, lsem):
    me = lax.axis_index("seq")
    load = pltpu.make_async_copy(w_hbm, w_ref, wsem)
    load.start()
    greet(n)

    def count_copy(step, src):
        peer = lax.rem(me + step, n)
        return pltpu.make_async_remote_copy(
            src_ref=count_ref, dst_ref=counts_ref.at[src], send_sem=csends.at[peer], recv_sem=crecvs.at[src],
            device_id={"seq": peer}, device_id_type=MESH,
        )

    def start_count(step, carry):
        count_copy(step, me).start()
        return carry

    lax.fori_loop(1, n, start_count, 0)
    counts_ref[me] = count_ref[...]
    x = emb_ref[...].astype(jnp.float32)
    x_ref[...] = (x * lax.rsqrt(jnp.mean(x * x, axis=-1, keepdims=True) + epsilon)).astype(jnp.bfloat16)
    load.wait()

    def copy_to(peer, src):
        return pltpu.make_async_remote_copy(
            src_ref=send.at[peer], dst_ref=recv_ref.at[src], send_sem=sends.at[peer], recv_sem=recvs.at[src],
            device_id={"seq": peer}, device_id_type=MESH,
        )

    def pair(step, carry):
        first = lax.rem(me // 2 + 1 + step, n // 2)
        block = w_ref[:, pl.ds(pl.multiple_of(first * 256, 256), 256)]
        out = jnp.dot(x_ref[...], block, preferred_element_type=jnp.float32).astype(jnp.bfloat16).T
        for e in range(2):
            head = first * 2 + e
            gate_ref[head] = out[e * 128:e * 128 + 32]
            send[head] = out[e * 128 + 32:e * 128 + 128]

            @pl.when(head != me)
            def _():
                copy_to(head, me).start()
        return carry

    lax.fori_loop(0, n // 2, pair, 0)
    own = pltpu.make_async_copy(send.at[me], recv_ref.at[me], lsem)
    own.start()
    own.wait()

    def finish(step, carry):
        source = lax.rem(me + n - step, n)
        peer = lax.rem(me + step, n)
        count_copy(step, me).wait_send()
        copy_to(peer, me).wait_send()
        count_copy(step, source).wait_recv()
        copy_to(peer, source).wait_recv()
        return carry

    lax.fori_loop(1, n, finish, 0)


def project(embedded, weight, count, n):
    tokens, width = embedded.shape
    bf = jnp.bfloat16
    vm = pl.BlockSpec(memory_space=pltpu.VMEM)
    hbm = pl.BlockSpec(memory_space=pl.ANY)
    return pl.pallas_call(
        functools.partial(project_kernel, n),
        out_shape=(
            jax.ShapeDtypeStruct((n, 32, tokens), bf),
            jax.ShapeDtypeStruct((n, 96, tokens), bf),
            jax.ShapeDtypeStruct((n, 8, 128), jnp.int32),
        ),
        in_specs=[vm, hbm, vm],
        out_specs=(vm, hbm, vm),
        scratch_shapes=[
            pltpu.VMEM(weight.shape, bf),
            pltpu.VMEM((tokens, width), bf),
            pltpu.VMEM((n, 96, tokens), bf),
            pltpu.SemaphoreType.DMA((n,)),
            pltpu.SemaphoreType.DMA((n,)),
            pltpu.SemaphoreType.DMA((n,)),
            pltpu.SemaphoreType.DMA((n,)),
            pltpu.SemaphoreType.DMA,
            pltpu.SemaphoreType.DMA,
        ],
        compiler_params=pltpu.CompilerParams(collective_id=1, has_side_effects=True, vmem_limit_bytes=40 << 20),
        name="project",
    )(embedded, weight, count)


def finish_kernel(n, att_ref, gate_ref, emb_ref, wo_hbm, up_hbm, down_hbm, out_ref, back, wo, up, down, sends, recvs, wsems, lsem):
    me = lax.axis_index("seq")
    loads = [
        pltpu.make_async_copy(wo_hbm, wo, wsems.at[0]),
        pltpu.make_async_copy(up_hbm, up, wsems.at[1]),
        pltpu.make_async_copy(down_hbm, down, wsems.at[2]),
    ]
    for load in loads:
        load.start()
    greet(n)

    def copy_to(peer, src):
        return pltpu.make_async_remote_copy(
            src_ref=att_ref.at[peer], dst_ref=back.at[src], send_sem=sends.at[peer], recv_sem=recvs.at[src],
            device_id={"seq": peer}, device_id_type=MESH,
        )

    def begin(step, carry):
        copy_to(lax.rem(me + step, n), me).start()
        return carry

    lax.fori_loop(1, n, begin, 0)
    back[me] = att_ref[me]
    for load in loads:
        load.wait()

    def finish(step, carry):
        source = lax.rem(me + n - step, n)
        peer = lax.rem(me + step, n)
        copy_to(peer, me).wait_send()
        copy_to(peer, source).wait_recv()
        return carry

    lax.fori_loop(1, n, finish, 0)
    rows = 128

    def tail(step, carry):
        span = pl.ds(pl.multiple_of(step * rows, rows), rows)
        att = back[:, :, span].reshape(n * 32, rows).astype(jnp.float32)
        gate = gate_ref[:, :, span].reshape(n * 32, rows).astype(jnp.float32)
        gate = gate / (1.0 + jnp.exp(-gate))
        scale = lax.rsqrt(jnp.mean(att * att, axis=0, keepdims=True) + epsilon)
        heads = (att * scale * gate).astype(jnp.bfloat16).T
        hidden = emb_ref[span, :].astype(jnp.float32) + jnp.dot(heads, wo[...], preferred_element_type=jnp.float32)
        normed = (hidden * lax.rsqrt(jnp.mean(hidden * hidden, axis=-1, keepdims=True) + epsilon)).astype(jnp.bfloat16)
        wide = jnp.dot(normed, up[...], preferred_element_type=jnp.float32)
        active = (wide / (1.0 + jnp.exp(-wide))).astype(jnp.bfloat16)
        out = hidden + jnp.dot(active, down[...], preferred_element_type=jnp.float32)
        out_ref[span, :] = out.astype(jnp.bfloat16)
        return carry

    lax.fori_loop(0, emb_ref.shape[0] // rows, tail, 0)


def finish_layer(attended, gate, embedded, wo, up, down, n):
    tokens, width = embedded.shape
    bf = jnp.bfloat16
    vm = pl.BlockSpec(memory_space=pltpu.VMEM)
    hbm = pl.BlockSpec(memory_space=pl.ANY)
    return pl.pallas_call(
        functools.partial(finish_kernel, n),
        out_shape=jax.ShapeDtypeStruct((tokens, width), bf),
        in_specs=[vm, vm, vm, hbm, hbm, hbm],
        out_specs=vm,
        scratch_shapes=[
            pltpu.VMEM((n, 32, tokens), bf),
            pltpu.VMEM(wo.shape, bf),
            pltpu.VMEM(up.shape, bf),
            pltpu.VMEM(down.shape, bf),
            pltpu.SemaphoreType.DMA((n,)),
            pltpu.SemaphoreType.DMA((n,)),
            pltpu.SemaphoreType.DMA((3,)),
            pltpu.SemaphoreType.DMA,
        ],
        compiler_params=pltpu.CompilerParams(collective_id=2, has_side_effects=True, vmem_limit_bytes=40 << 20),
        name="finish",
    )(attended, gate, embedded, wo, up, down)


def local(token_rows, segment_ids, requests, hot_table, cold_table, input_weight, output_weight, up_weight, down_weight):
    seq_devices = lax.axis_size("seq")
    all_devices = lax.axis_size("emb") * seq_devices
    capacity = requests.shape[2]
    hot_count, model_width = hot_table.shape
    tokens_here = token_rows.shape[1]
    head_width = model_width // H
    below = jnp.sum(segment_ids[0][None, :] < jnp.arange(1, 4, dtype=jnp.int32)[:, None], axis=1, dtype=jnp.int32)
    count = jnp.broadcast_to(jnp.pad(below, (0, 125))[None], (8, 128))
    fetched = lax.all_to_all(
        cold_table[lax.all_to_all(requests[0], ("emb", "seq"), split_axis=0, concat_axis=0, tiled=True)],
        ("emb", "seq"), split_axis=0, concat_axis=0, tiled=True,
    ).reshape(all_devices * capacity, model_width)
    item_ids = token_rows[0]
    is_hot = item_ids < hot_count
    hot_rows = hot_table[jnp.where(is_hot, item_ids, 0)]
    cold_rows = fetched[jnp.where(is_hot, 0, item_ids - hot_count)]
    embedded = jnp.where(is_hot[:, None], hot_rows, cold_rows)
    gate, triples, counts = project(embedded, input_weight, count, seq_devices)
    starts = jnp.sum(counts[:, 0, :4], axis=0, dtype=jnp.int32)
    attended = attention(starts, triples, 512, 512, 2, True)
    return finish_layer(attended, gate, embedded, output_weight, up_weight, down_weight, seq_devices)[None]


def solution(mesh):
    placed = (
        P("emb", "seq"), P("emb", "seq"), P(("emb", "seq"), None, None), P(), P(("emb", "seq"), None), P(), P(), P(), P(),
    )
    return jax.shard_map(local, mesh=mesh, in_specs=placed, out_specs=P("emb", "seq", None), check_vma=False)
```

time: 306 us -> 127 us (0.42)
  matrix products: 96.7 us -> 0 us
  Pallas kernels: 0 us -> 66.5 us
  waiting for transfers between devices: 78 us -> 16.9 us
  local copies, waits for them, and re-layouts: 61.1 us -> 23.6 us
  blocking collectives: 20.5 us -> 0 us
  between operations: 13.6 us -> 0.15 us
  other arithmetic: 14.7 us -> 2.79 us
  loops' own time: 5.8 us -> 0 us
    dot_general x13 -> x0, matrix products: 95.2 us -> none  [the longest x10 82.4 us: add_keys(): jnp.einsum('gqk,kgc->qgc', weights, value_block, preferred_element_type=j...]
    pallas_call x0 -> x3, Pallas kernels: none -> 66.5 us  [the longest x1 25.2 us: project(): pl.pallas_call(functools.partial(project_kernel, n), out_shape=(jax.Shape...]
    all_gather x1 -> x0, waiting for transfers between devices: 61.5 us -> none  [local(): lax.all_gather(normed_input, 'seq', axis=0, tiled=True)]
    all_to_all x1 -> x0, blocking collectives: 20.5 us -> none  [local(): lax.all_to_all(requested, ('emb', 'seq'), split_axis=0, concat_axis=0, ti...]
    unnamed x21 -> x16, local copies, waits for them, and re-layouts: 14.4 us -> 7.62 us
    convert_element_type x2 -> x0, local copies, waits for them, and re-layouts: 6.41 us -> none  [local(): returned.reshape(seq_devices, tokens_here, head_groups, head_width)]
    all_to_all x2 -> x0, local copies, waits for them, and re-layouts: 6.01 us -> none  [local(): lax.all_to_all(attended.reshape(seq_devices, tokens_here * head_groups *...]
    another operation x5 -> x0, loops' own time: 5.8 us -> none  [the longest x1 5.31 us: attend(): lax.map(one_block, (query_blocks, segment_blocks, jnp.arange(blocks, dtyp...]
  transfers between devices with their start and end apart: 4 -> 2, of which waited for: 4 -> 2; matrix products, arithmetic and copies ran while one was open for 5% -> 4% of each run, Pallas kernels for 0% -> 0%
where the time goes in v1:
time: 127 us
  Pallas kernels  66.5 us (52%)
  local copies, waits for them, and re-layouts  23.6 us (19%)
  starting transfers between devices  16.9 us (13%)
  waiting for transfers between devices  16.9 us (13%)
  other arithmetic  2.79 us (2%)
    pallas_call x1, Pallas kernels, project(): pl.pallas_call(functools.partial(project_kernel, n), out_shape=(jax.Shape...  25.2 us
    pallas_call x1, Pallas kernels, attention(): pl.pallas_call(functools.partial(attn_kernel, TQ, TK, U, BF), out_shape=j...  24.4 us
    pallas_call x1, Pallas kernels, finish_layer(): pl.pallas_call(functools.partial(finish_kernel, n), out_shape=jax.ShapeDt...  17 us
    all_to_all x1, starting transfers between devices, local(): lax.all_to_all(requests[0], ('emb', 'seq'), split_axis=0, concat_axis=0,...  11.2 us
    all_to_all x1, waiting for transfers between devices, local(): lax.all_to_all(requests[0], ('emb', 'seq'), split_axis=0, concat_axis=0,...  8.55 us
    all_to_all x1, waiting for transfers between devices, local(): lax.all_to_all(cold_table[lax.all_to_all(requests[0], ('emb', 'seq'), spl...  8.34 us
    unnamed x16, local copies, waits for them, and re-layouts  7.62 us
    gather x2, local copies, waits for them, and re-layouts, local(): cold_table[lax.all_to_all(requests[0], ('emb', 'seq'), split_axis=0, conc...  7.36 us
  transfers between devices with their start and end apart: 2, of which 2 were waited for; matrix products, arithmetic and copies ran while one was open for 4% of the time, Pallas kernels for 0%

profile of v1, /device:TPU:0, one launch (start us, length us, event | category | flops | bytes accessed | tf_op | source)
XLA Modules:
  0.0 126.9 jit_solution(17726535514341963092)
XLA Ops:
  0.0 0.0 copy-start.6
  0.0 1.4 %copy.12 = s32[1,128,4]{2,1,0:T(8,128)} copy(s32[1,128,4]{1,2,0:T(4,128)} %param.11) | data formatting | bytes 4096 | tf_op args[2]
  1.4 11.2 %all-to-all-start = ((s32[128,1,4]{2,1,0:T(1,128)}), s32[128,1,4]{2,1,0:T(1,128)S(1)}, u32[]{:S(2)}, u32[]{:S(2)}) async-start(s32[128,1,4]{2,1,0:T(1,128)} %bitcast.2), calls=%async_computation | async-start | bytes 131072 | tf_op jit(solution)/shard_map/all_to_all | solution.py:354
  12.6 0.9 convert_reduce_fusion
  13.5 8.6 %all-to-all-done = s32[128,1,4]{2,1,0:T(1,128)S(1)} async-done(((s32[128,1,4]{2,1,0:T(1,128)}), s32[128,1,4]{2,1,0:T(1,128)S(1)}, u32[]{:S(2)}, u32[]{:S(2)}) %all-to-all-start) | async-done | bytes 2080 | tf_op jit(solution)/shard_map/all_to_all | solution.py:354
  22.1 0.1 reshape.108
  22.2 6.4 %gather_fusion.1 = bf16[512,512]{1,0:T(8,128)(2,1)S(1)} fusion(bf16[8192,512]{1,0:T(8,128)(2,1)} %param.13, s32[1024]{0:T(1024)S(1)} %pad_clamp_fusion.1), kind=kCustom, calls=%fused_computation.1 | custom fusion | bytes 1050624 | tf_op jit(solution)/shard_map/gather | solution.py:354
  28.6 0.9 reshape.107
  29.6 5.7 %all-to-all-start.1 = ((bf16[128,4,512]{2,1,0:T(4,128)(2,1)}), bf16[128,4,512]{2,1,0:T(4,128)(2,1)}, u32[]{:S(2)}, u32[]{:S(2)}) async-start(bf16[128,4,512]{2,1,0:T(4,128)(2,1)} %reshape.107), calls=%async_computation.1 | async-start | bytes 1048576 | tf_op jit(solution)/shard_map/all_to_all | solution.py:353
  35.3 0.0 copy-done.6
  35.3 4.7 %gather_fusion = bf16[512,512]{1,0:T(8,128)(2,1)S(1)} fusion(bf16[4096,512]{1,0:T(8,128)(2,1)} %param.12, s32[1024]{0:T(1024)S(1)} %pad_clamp_fusion.2), kind=kCustom, calls=%fused_computation | custom fusion | bytes 1050624 | tf_op jit(solution)/shard_map/gather | solution.py:359
  40.1 0.0 copy-start
  40.1 8.3 %all-to-all-done.1 = bf16[128,4,512]{2,1,0:T(4,128)(2,1)} async-done(((bf16[128,4,512]{2,1,0:T(4,128)(2,1)}), bf16[128,4,512]{2,1,0:T(4,128)(2,1)}, u32[]{:S(2)}, u32[]{:S(2)}) %all-to-all-start.1) | async-done | bytes 524320 | tf_op jit(solution)/shard_map/all_to_all | solution.py:353
  48.5 1.2 reshape.97
  49.6 2.6 %gather_fusion.2 = bf16[512,512]{1,0:T(8,128)(2,1)} fusion(bf16[512,512]{1,0:T(8,128)(2,1)S(1)} %reshape.97, s32[1024]{0:T(1024)S(1)} %pad_clamp_fusion), kind=kCustom, calls=%fused_computation.2 | custom fusion | bytes 1050624 | tf_op jit(solution)/shard_map/gather | solution.py:360
  52.3 0.0 copy-start.5
  52.3 1.2 broadcast_select_fusion.emb_ref
  53.5 0.0 copy-done
  53.5 25.2 %project.1 = (bf16[16,32,512]{2,1,0:T(8,128)(2,1)S(1)}, bf16[16,96,512]{2,1,0:T(8,128)(2,1)S(1)}, s32[16,8,128]{2,1,0:T(8,128)S(1)}) custom-call(bf16[512,512]{1,0:T(8,128)(2,1)S(1)} %broadcast_select_fusion.emb_ref, bf16[512,2048]{1,0:T(8,128)(2,1)S(1)} %copy-done, s32[8,128]{1,0:T(8,128)S(1)} %broadcast_in_dim.30.count_ref), custom_call_target="tpu_custom_call" | custom-call | tf_op jit(solution)/shard_map/project/pallas_call | solution.py:240
  78.7 0.0 copy-start.4
  78.7 1.2 copy-done.4
  79.9 0.6 slice_reduce_fusion.starts_ref
  80.5 24.4 %attn.1.att_ref = bf16[16,32,512]{2,1,0:T(8,128)(2,1)} custom-call(s32[4]{0:T(128)} %slice_reduce_fusion.starts_ref, bf16[16,96,512]{2,1,0:T(8,128)(2,1)} %copy-done.4), custom_call_target="tpu_custom_call" | custom-call | tf_op jit(solution)/shard_map/attn/pallas_call | solution.py:141
  104.9 0.0 copy-done.5
  104.9 0.0 copy-start.1
  104.9 1.6 %copy-done.1 = bf16[512,2048]{1,0:T(8,128)(2,1)S(1)} copy-done((bf16[512,2048]{1,0:T(8,128)(2,1)S(1)}, bf16[512,2048]{1,0:T(8,128)(2,1)}, u32[]{:S(2)}) %copy-start.1) | copy-done | bytes 2097176
  106.5 0.0 copy-start.2
  106.5 1.6 %copy-done.2 = bf16[2048,512]{1,0:T(8,128)(2,1)S(1)} copy-done((bf16[2048,512]{1,0:T(8,128)(2,1)S(1)}, bf16[2048,512]{1,0:T(8,128)(2,1)}, u32[]{:S(2)}) %copy-start.2) | copy-done | bytes 2097176
  108.1 0.0 copy-start.3
  108.1 1.0 copy-done.3
  109.1 17.0 %finish.1 = bf16[512,512]{1,0:T(8,128)(2,1)S(1)} custom-call(bf16[16,32,512]{2,1,0:T(8,128)(2,1)S(1)} %copy-done.3, bf16[16,32,512]{2,1,0:T(8,128)(2,1)S(1)} %get-tuple-element.10.gate_ref, bf16[512,512]{1,0:T(8,128)(2,1)S(1)} %broadcast_select_fusion.emb_ref, bf16[512,512]{1,0:T(8,128)(2,1)S(1)} %copy-done.5, bf16[512,2048]{1,0:T(8,128)(2,1)S(1)} %copy-done.1, ...), custom_call_target="tpu_custom_call" | custom-call | tf_op jit(solution)/shard_map/finish/pallas_call | solution.py:324
  126.1 0.8 copy.14
  (9 shorter events, 0.1 us)
Async XLA Ops:
  0.0 35.3 %copy-start.6 = (s32[1,512]{1,0:T(1,128)S(1)}, s32[1,512]{1,0:T(1,128)}, u32[]{:S(2)}) copy-start(s32[1,512]{1,0:T(1,128)} %param.9) | copy-start | bytes 6148
  1.4 20.6 %all-to-all-start = ((s32[128,1,4]{2,1,0:T(1,128)}), s32[128,1,4]{2,1,0:T(1,128)S(1)}, u32[]{:S(2)}, u32[]{:S(2)}) async-start(s32[128,1,4]{2,1,0:T(1,128)} %bitcast.2), calls=%async_computation | async-start | bytes 131072 | tf_op jit(solution)/shard_map/all_to_all | solution.py:354
  29.6 18.9 %all-to-all-start.1 = ((bf16[128,4,512]{2,1,0:T(4,128)(2,1)}), bf16[128,4,512]{2,1,0:T(4,128)(2,1)}, u32[]{:S(2)}, u32[]{:S(2)}) async-start(bf16[128,4,512]{2,1,0:T(4,128)(2,1)} %reshape.107), calls=%async_computation.1 | async-start | bytes 1048576 | tf_op jit(solution)/shard_map/all_to_all | solution.py:353
  40.1 13.4 %copy-start = (bf16[512,2048]{1,0:T(8,128)(2,1)S(1)}, bf16[512,2048]{1,0:T(8,128)(2,1)}, u32[]{:S(2)}) copy-start(bf16[512,2048]{1,0:T(8,128)(2,1)} %w_hbm.1) | copy-start | bytes 6291460
  52.3 52.6 %copy-start.5 = (bf16[512,512]{1,0:T(8,128)(2,1)S(1)}, bf16[512,512]{1,0:T(8,128)(2,1)}, u32[]{:S(2)}) copy-start(bf16[512,512]{1,0:T(8,128)(2,1)} %wo_hbm.1) | copy-start | bytes 1572868
  78.7 1.2 copy-start.4
  104.9 1.6 %copy-start.1 = (bf16[512,2048]{1,0:T(8,128)(2,1)S(1)}, bf16[512,2048]{1,0:T(8,128)(2,1)}, u32[]{:S(2)}) copy-start(bf16[512,2048]{1,0:T(8,128)(2,1)} %up_hbm.1) | copy-start | bytes 6291460
  106.5 1.6 %copy-start.2 = (bf16[2048,512]{1,0:T(8,128)(2,1)S(1)}, bf16[2048,512]{1,0:T(8,128)(2,1)}, u32[]{:S(2)}) copy-start(bf16[2048,512]{1,0:T(8,128)(2,1)} %down_hbm.1) | copy-start | bytes 6291460
  108.1 1.0 copy-start.3

commit v2 on v1

--- a/solution.py
+++ b/solution.py
@@ -1,5 +1,4 @@
 import functools
-import math
 
 import jax
 import jax.numpy as jnp
@@ -8,16 +7,18 @@
 from jax.experimental.pallas import tpu as pltpu
 from jax.sharding import PartitionSpec as P
 
-H = 16
 epsilon = 1e-06
 
 BIG = float(2 ** 30)
 
-def attn_kernel(TQ, TK, U, BF, starts_ref, qkv_ref, out_ref, q_scr, k_scr, v_scr, m_scr, a_scr, acc_scr):
+def attn_kernel(TQ, TK, U, BF, segs_ref, qkv_ref, out_ref, q_scr, k_scr, v_scr, m_scr, a_scr, acc_scr):
     nb, _, W = qkv_ref.shape
     L = nb * W
     NQ = L // TQ
-    s1, s2, s3 = starts_ref[0], starts_ref[1], starts_ref[2]
+    segments = segs_ref[...]
+    s1, s2, s3 = [
+        jnp.sum((segments < s).astype(jnp.float32)).astype(jnp.int32) for s in (1, 2, 3)
+    ]
     C = 0.5 / (32.0 ** 0.5)
     bf = jnp.bfloat16
 
@@ -133,7 +134,7 @@
     lax.fori_loop(0, steps, body, (i0, j0, i1, j1))
 
 
-def attention(starts, qkv, TQ=512, TK=512, U=1, BF=True):
+def attention(segs, qkv, TQ=512, TK=512, U=1, BF=True):
     nb, _, W = qkv.shape
     L = nb * W
     bf = jnp.bfloat16
@@ -141,7 +142,7 @@
     return pl.pallas_call(
         functools.partial(attn_kernel, TQ, TK, U, BF),
         out_shape=jax.ShapeDtypeStruct((nb, 32, W), bf),
-        in_specs=[pl.BlockSpec(memory_space=pltpu.SMEM), pl.BlockSpec(memory_space=pltpu.VMEM)],
+        in_specs=[pl.BlockSpec(memory_space=pltpu.VMEM), pl.BlockSpec(memory_space=pltpu.VMEM)],
         out_specs=pl.BlockSpec(memory_space=pltpu.VMEM),
         scratch_shapes=[
             pltpu.VMEM((L // 256, 48, 256), bf),
@@ -153,47 +154,163 @@
         ],
         compiler_params=pltpu.CompilerParams(vmem_limit_bytes=60 << 20),
         name="attn",
-    )(starts, qkv)
+    )(segs, qkv)
 
 
 MESH = pl.DeviceIdType.MESH
 
 
-def greet(axis_size):
-    me = lax.axis_index("seq")
+def one_hot(ids, base, width):
+    lane = lax.broadcasted_iota(jnp.int32, ids.shape, 1).astype(jnp.float32)
+    pieces = [
+        jnp.where(ids == lane + (base + 128 * c), 1.0, 0.0).astype(jnp.bfloat16) for c in range(width // 128)
+    ]
+    return jnp.concatenate(pieces, axis=1)
+
+
+def front_kernel(
+    n, m, tok_ref, seg_ref, req_ref, hot_hbm, cold_hbm, w_hbm, emb_ref, gate_ref, recv_ref, segs_ref,
+    hot, cold, w_ref, x_ref, send, asks, asked, rows_out, rows_in, acc, gat, tokb, idx, flat,
+    sends, recvs, msems, lsems,
+):
+    me_s = lax.axis_index("seq")
+    me = lax.axis_index("emb") * n + me_s
+    total = n * m
+    bf = jnp.bfloat16
+    f32 = jnp.float32
+    hot_count = hot_hbm.shape[0]
+    cold_count = cold_hbm.shape[0]
+    step_rows = 512
+
     barrier = pltpu.get_barrier_semaphore()
 
+    def device(peer):
+        return {"emb": peer // n, "seq": lax.rem(peer, n)}
+
     def signal(step, carry):
-        peer = lax.rem(me + step, axis_size)
-        pl.semaphore_signal(barrier, inc=1, device_id={"seq": peer}, device_id_type=MESH)
-        return carry
-
-    lax.fori_loop(1, axis_size, signal, 0)
-    pl.semaphore_wait(barrier, axis_size - 1)
-
-
-def project_kernel(n, emb_ref, w_hbm, count_ref, gate_ref, recv_ref, counts_ref, w_ref, x_ref, send, sends, recvs, csends, crecvs, wsem, lsem):
-    me = lax.axis_index("seq")
-    load = pltpu.make_async_copy(w_hbm, w_ref, wsem)
-    load.start()
-    greet(n)
-
-    def count_copy(step, src):
-        peer = lax.rem(me + step, n)
+        peer = lax.rem(me + step, total)
+        pl.semaphore_signal(barrier, inc=1, device_id=device(peer), device_id_type=MESH)
+        return carry
+
+    lax.fori_loop(1, total, signal, 0)
+    hot_load = pltpu.make_async_copy(hot_hbm, hot, lsems.at[0])
+    cold_load = pltpu.make_async_copy(cold_hbm, cold, lsems.at[1])
+    w_load = pltpu.make_async_copy(w_hbm, w_ref, lsems.at[2])
+    hot_load.start()
+    cold_load.start()
+    w_load.start()
+    wanted = req_ref[0].astype(f32)
+    wanted = jnp.concatenate([wanted, jnp.zeros((total - wanted.shape[0], total), f32)], axis=0).T
+    asks[...] = wanted.reshape(total, 1, total)
+    tokb[...] = jnp.broadcast_to(tok_ref[...].astype(f32), (128, tok_ref.shape[1])).T
+    pl.semaphore_wait(barrier, total - 1)
+
+    def ask(peer, src):
         return pltpu.make_async_remote_copy(
-            src_ref=count_ref, dst_ref=counts_ref.at[src], send_sem=csends.at[peer], recv_sem=crecvs.at[src],
-            device_id={"seq": peer}, device_id_type=MESH,
+            src_ref=asks.at[peer], dst_ref=asked.at[src], send_sem=msems.at[0], recv_sem=msems.at[1],
+            device_id=device(peer), device_id_type=MESH,
         )
 
-    def start_count(step, carry):
-        count_copy(step, me).start()
-        return carry
-
-    lax.fori_loop(1, n, start_count, 0)
-    counts_ref[me] = count_ref[...]
-    x = emb_ref[...].astype(jnp.float32)
-    x_ref[...] = (x * lax.rsqrt(jnp.mean(x * x, axis=-1, keepdims=True) + epsilon)).astype(jnp.bfloat16)
-    load.wait()
+    def start_ask(step, carry):
+        ask(lax.rem(me + step, total), me).start()
+        return carry
+
+    lax.fori_loop(1, total, start_ask, 0)
+
+    def seg_copy(step, src):
+        return pltpu.make_async_remote_copy(
+            src_ref=seg_ref, dst_ref=segs_ref.at[src], send_sem=msems.at[4], recv_sem=recvs.at[n + src],
+            device_id={"seq": lax.rem(me_s + step, n)}, device_id_type=MESH,
+        )
+
+    asked[me] = asks[me]
+    segs_ref[me_s] = seg_ref[...]
+
+    hot_load.wait()
+    acc[...] = jnp.zeros_like(acc)
+
+    def add_hot(step, carry):
+        base = step * step_rows
+        pick = one_hot(tokb[...], base.astype(f32), step_rows)
+        block = hot[pl.ds(pl.multiple_of(base, step_rows), step_rows), :]
+        acc[...] += jnp.dot(pick, block, preferred_element_type=f32)
+        return carry
+
+    lax.fori_loop(0, hot_count // step_rows, add_hot, 0)
+
+    every = pl.ds(0, total - 1)
+
+    def all_of(src, dst, a, b):
+        return pltpu.make_async_remote_copy(
+            src_ref=src.at[every], dst_ref=dst.at[every], send_sem=msems.at[a], recv_sem=msems.at[b],
+            device_id=device(me), device_id_type=MESH,
+        )
+
+    all_of(asks, asked, 0, 1).wait_recv()
+    ids = asked[...].reshape(total, 128)
+    high = jnp.floor(ids * (1.0 / 64.0))
+    low = ids - high * 64.0
+    slots = idx.shape[0]
+    slot = lax.broadcasted_iota(jnp.int32, (slots, 128), 0)
+    lane = lax.broadcasted_iota(jnp.int32, (slots, 128), 1)
+    spread = jnp.where(slot // 4 == lane, 1.0, 0.0).astype(bf)
+    ids = 64.0 * jnp.dot(spread, high.astype(bf), preferred_element_type=f32) + jnp.dot(
+        spread, low.astype(bf), preferred_element_type=f32
+    )
+    ids = jnp.sum(jnp.where(lax.rem(slot, 4) == lane, ids, 0.0), axis=1, keepdims=True)
+    idx[...] = jnp.broadcast_to(ids, (slots, 128))
+    cold_load.wait()
+
+    def give(peer, src):
+        return pltpu.make_async_remote_copy(
+            src_ref=rows_out.at[peer], dst_ref=rows_in.at[src], send_sem=msems.at[2], recv_sem=msems.at[3],
+            device_id=device(peer), device_id_type=MESH,
+        )
+
+    half = slots // 2
+
+    def serve(part, carry):
+        gat[...] = jnp.zeros_like(gat)
+        mine = idx[pl.ds(pl.multiple_of(part * half, half), half), :]
+
+        def add_cold(step, inner):
+            base = step * step_rows
+            pick = one_hot(mine, base.astype(f32), step_rows)
+            block = cold[pl.ds(pl.multiple_of(base, step_rows), step_rows), :]
+            gat[...] += jnp.dot(pick, block, preferred_element_type=f32)
+            return inner
+
+        lax.fori_loop(0, cold_count // step_rows, add_cold, 0)
+        rows_out[pl.ds(part * (total // 2), total // 2)] = gat[...].astype(bf).reshape(total // 2, 4, gat.shape[1])
+
+        def start_give(step, inner):
+            peer = part * (total // 2) + lax.rem(me + step, total // 2)
+
+            @pl.when(peer != me)
+            def _():
+                give(peer, me).start()
+            return inner
+
+        lax.fori_loop(0, total // 2, start_give, 0)
+        return carry
+
+    lax.fori_loop(0, 2, serve, 0)
+    rows_in[me] = rows_out[me]
+    all_of(asks, asked, 0, 1).wait_send()
+
+    def start_seg(step, carry):
+        seg_copy(step, me_s).start()
+        return carry
+
+    lax.fori_loop(1, n, start_seg, 0)
+    all_of(rows_out, rows_in, 2, 3).wait_recv()
+    flat[...] = rows_in[...].reshape(flat.shape)
+    pick = one_hot(tokb[...], float(hot_count), slots)
+    found = (acc[...] + jnp.dot(pick, flat[...], preferred_element_type=f32)).astype(bf)
+    emb_ref[...] = found
+    x = found.astype(f32)
+    x_ref[...] = (x * lax.rsqrt(jnp.mean(x * x, axis=-1, keepdims=True) + epsilon)).astype(bf)
+    w_load.wait()
 
     def copy_to(peer, src):
         return pltpu.make_async_remote_copy(
@@ -202,64 +319,95 @@
         )
 
     def pair(step, carry):
-        first = lax.rem(me // 2 + 1 + step, n // 2)
+        first = lax.rem(me_s // 2 + 1 + step, n // 2)
         block = w_ref[:, pl.ds(pl.multiple_of(first * 256, 256), 256)]
-        out = jnp.dot(x_ref[...], block, preferred_element_type=jnp.float32).astype(jnp.bfloat16).T
+        out = jnp.dot(x_ref[...], block, preferred_element_type=f32).astype(bf).T
         for e in range(2):
             head = first * 2 + e
             gate_ref[head] = out[e * 128:e * 128 + 32]
             send[head] = out[e * 128 + 32:e * 128 + 128]
 
-            @pl.when(head != me)
+            @pl.when(head != me_s)
             def _():
-                copy_to(head, me).start()
+                copy_to(head, me_s).start()
         return carry
 
     lax.fori_loop(0, n // 2, pair, 0)
-    own = pltpu.make_async_copy(send.at[me], recv_ref.at[me], lsem)
+    own = pltpu.make_async_copy(send.at[me_s], recv_ref.at[me_s], lsems.at[3])
     own.start()
+    all_of(rows_out, rows_in, 2, 3).wait_send()
     own.wait()
 
     def finish(step, carry):
-        source = lax.rem(me + n - step, n)
-        peer = lax.rem(me + step, n)
-        count_copy(step, me).wait_send()
-        copy_to(peer, me).wait_send()
-        count_copy(step, source).wait_recv()
+        source = lax.rem(me_s + n - step, n)
+        peer = lax.rem(me_s + step, n)
+        copy_to(peer, me_s).wait_send()
+        seg_copy(step, source).wait_recv()
         copy_to(peer, source).wait_recv()
         return carry
 
     lax.fori_loop(1, n, finish, 0)
-
-
-def project(embedded, weight, count, n):
-    tokens, width = embedded.shape
+    pltpu.make_async_remote_copy(
+        src_ref=segs_ref.at[pl.ds(0, n - 1)], dst_ref=segs_ref.at[pl.ds(0, n - 1)], send_sem=msems.at[4],
+        recv_sem=msems.at[4], device_id=device(me), device_id_type=MESH,
+    ).wait_send()
+
+
+def front(token_rows, segment_ids, requests, hot_table, cold_table, weight, n, m):
+    tokens = token_rows.shape[1]
+    width = hot_table.shape[1]
+    total = n * m
+    slots = total * requests.shape[1]
     bf = jnp.bfloat16
+    f32 = jnp.float32
     vm = pl.BlockSpec(memory_space=pltpu.VMEM)
-    hbm = pl.BlockSpec(memory_space=pl.ANY)
+    hbm = pl.BlockSpec(memory_space=pltpu.HBM)
     return pl.pallas_call(
-        functools.partial(project_kernel, n),
+        functools.partial(front_kernel, n, m),
         out_shape=(
+            jax.ShapeDtypeStruct((tokens, width), bf),
             jax.ShapeDtypeStruct((n, 32, tokens), bf),
             jax.ShapeDtypeStruct((n, 96, tokens), bf),
-            jax.ShapeDtypeStruct((n, 8, 128), jnp.int32),
+            jax.ShapeDtypeStruct((n, 1, tokens), jnp.int32),
         ),
-        in_specs=[vm, hbm, vm],
-        out_specs=(vm, hbm, vm),
+        in_specs=[vm, vm, vm, hbm, hbm, hbm],
+        out_specs=(vm, vm, hbm, vm),
         scratch_shapes=[
+            pltpu.VMEM(hot_table.shape, bf),
+            pltpu.VMEM(cold_table.shape, bf),
             pltpu.VMEM(weight.shape, bf),
             pltpu.VMEM((tokens, width), bf),
             pltpu.VMEM((n, 96, tokens), bf),
+            pltpu.VMEM((total, 1, 128), f32),
+            pltpu.VMEM((total, 1, 128), f32),
+            pltpu.VMEM((total, 4, width), bf),
+            pltpu.VMEM((total, 4, width), bf),
+            pltpu.VMEM((tokens, width), f32),
+            pltpu.VMEM((slots // 2, width), f32),
+            pltpu.VMEM((tokens, 128), f32),
+            pltpu.VMEM((slots, 128), f32),
+            pltpu.VMEM((slots, width), bf),
             pltpu.SemaphoreType.DMA((n,)),
-            pltpu.SemaphoreType.DMA((n,)),
-            pltpu.SemaphoreType.DMA((n,)),
-            pltpu.SemaphoreType.DMA((n,)),
-            pltpu.SemaphoreType.DMA,
-            pltpu.SemaphoreType.DMA,
+            pltpu.SemaphoreType.DMA((2 * n,)),
+            pltpu.SemaphoreType.DMA((5,)),
+            pltpu.SemaphoreType.DMA((4,)),
         ],
-        compiler_params=pltpu.CompilerParams(collective_id=1, has_side_effects=True, vmem_limit_bytes=40 << 20),
-        name="project",
-    )(embedded, weight, count)
+        compiler_params=pltpu.CompilerParams(collective_id=1, has_side_effects=True, vmem_limit_bytes=50 << 20),
+        name="front",
+    )(token_rows, segment_ids, requests, hot_table, cold_table, weight)
+
+
+def greet(axis_size):
+    me = lax.axis_index("seq")
+    barrier = pltpu.get_barrier_semaphore()
+
+    def signal(step, carry):
+        peer = lax.rem(me + step, axis_size)
+        pl.semaphore_signal(barrier, inc=1, device_id={"seq": peer}, device_id_type=MESH)
+        return carry
+
+    lax.fori_loop(1, axis_size, signal, 0)
+    pl.semaphore_wait(barrier, axis_size - 1)
 
 
 def finish_kernel(n, att_ref, gate_ref, emb_ref, wo_hbm, up_hbm, down_hbm, out_ref, back, wo, up, down, sends, recvs, wsems, lsem):
@@ -320,7 +468,7 @@
     tokens, width = embedded.shape
     bf = jnp.bfloat16
     vm = pl.BlockSpec(memory_space=pltpu.VMEM)
-    hbm = pl.BlockSpec(memory_space=pl.ANY)
+    hbm = pl.BlockSpec(memory_space=pltpu.HBM)
     return pl.pallas_call(
         functools.partial(finish_kernel, n),
         out_shape=jax.ShapeDtypeStruct((tokens, width), bf),
@@ -342,27 +490,13 @@
 
 
 def local(token_rows, segment_ids, requests, hot_table, cold_table, input_weight, output_weight, up_weight, down_weight):
-    seq_devices = lax.axis_size("seq")
-    all_devices = lax.axis_size("emb") * seq_devices
-    capacity = requests.shape[2]
-    hot_count, model_width = hot_table.shape
-    tokens_here = token_rows.shape[1]
-    head_width = model_width // H
-    below = jnp.sum(segment_ids[0][None, :] < jnp.arange(1, 4, dtype=jnp.int32)[:, None], axis=1, dtype=jnp.int32)
-    count = jnp.broadcast_to(jnp.pad(below, (0, 125))[None], (8, 128))
-    fetched = lax.all_to_all(
-        cold_table[lax.all_to_all(requests[0], ("emb", "seq"), split_axis=0, concat_axis=0, tiled=True)],
-        ("emb", "seq"), split_axis=0, concat_axis=0, tiled=True,
-    ).reshape(all_devices * capacity, model_width)
-    item_ids = token_rows[0]
-    is_hot = item_ids < hot_count
-    hot_rows = hot_table[jnp.where(is_hot, item_ids, 0)]
-    cold_rows = fetched[jnp.where(is_hot, 0, item_ids - hot_count)]
-    embedded = jnp.where(is_hot[:, None], hot_rows, cold_rows)
-    gate, triples, counts = project(embedded, input_weight, count, seq_devices)
-    starts = jnp.sum(counts[:, 0, :4], axis=0, dtype=jnp.int32)
-    attended = attention(starts, triples, 512, 512, 2, True)
-    return finish_layer(attended, gate, embedded, output_weight, up_weight, down_weight, seq_devices)[None]
+    n = lax.axis_size("seq")
+    m = lax.axis_size("emb")
+    embedded, gate, triples, segments = front(
+        token_rows, segment_ids, jnp.transpose(requests, (0, 2, 1)), hot_table, cold_table, input_weight, n, m
+    )
+    attended = attention(segments, triples, 512, 512, 2, True)
+    return finish_layer(attended, gate, embedded, output_weight, up_weight, down_weight, n)[None]
 
 
 def solution(mesh):

time: 127 us -> 111 us (0.87)
  the two profiles are of different devices: /device:TPU:0 before, /device:TPU:4 now
where the time goes in v2:
time: 111 us; the launch traced here: 110 us
  Pallas kernels  103 us (93%)
  local copies, waits for them, and re-layouts  7.22 us (7%)
    pallas_call x1, Pallas kernels, front(): pl.pallas_call(functools.partial(front_kernel, n, m), out_shape=(jax.Shap...  60.4 us
    pallas_call x1, Pallas kernels, attention(): pl.pallas_call(functools.partial(attn_kernel, TQ, TK, U, BF), out_shape=j...  23.6 us
    pallas_call x1, Pallas kernels, finish_layer(): pl.pallas_call(functools.partial(finish_kernel, n), out_shape=jax.ShapeDt...  19 us
    unnamed x19, local copies, waits for them, and re-layouts  7.22 us

profile of v2, /device:TPU:4, one launch (start us, length us, event | category | flops | bytes accessed | tf_op | source)
XLA Modules:
  0.0 110.2 jit_solution(10516094733449100762)
XLA Ops:
  0.0 0.0 copy-start.6
  0.0 0.7 copy-done.6
  0.7 0.0 copy-start.7
  0.7 0.7 copy-done.7
  1.4 0.0 copy-start.8
  1.4 0.7 copy-done.8
  2.0 0.0 copy-start.4
  2.0 60.4 %front.1 = (bf16[512,512]{1,0:T(8,128)(2,1)S(1)}, bf16[16,32,512]{2,1,0:T(8,128)(2,1)S(1)}, bf16[16,96,512]{2,1,0:T(8,128)(2,1)S(1)}, s32[16,1,512]{2,1,0:T(1,128)S(1)}) custom-call(s32[1,512]{1,0:T(1,128)S(1)} %copy-done.6, s32[1,512]{1,0:T(1,128)S(1)} %copy-done.7, s32[1,4,128]{2,1,0:T(4,128)S(1)} %bitcast.3, bf16[4096,512]{1,0:T(8,128)(2,1)} %hot_hbm.1, ...), custom_call_target="tpu_custom_call" | custom-call | tf_op jit(solution)/shard_map/front/pallas_call | solution.py:365
  62.4 0.0 copy-start.3
  62.5 1.1 %copy-done.3 = bf16[16,96,512]{2,1,0:T(8,128)(2,1)} copy-done((bf16[16,96,512]{2,1,0:T(8,128)(2,1)}, bf16[16,96,512]{2,1,0:T(8,128)(2,1)S(1)}, u32[]{:S(2)}) %copy-start.3) | copy-done | bytes 1572888
  63.6 0.0 copy-start.5
  63.6 0.6 copy-done.5
  64.2 0.0 copy-start
  64.2 23.6 %attn.1.att_ref = bf16[16,32,512]{2,1,0:T(8,128)(2,1)} custom-call(s32[16,1,512]{2,1,0:T(1,128)} %copy-done.5, bf16[16,96,512]{2,1,0:T(8,128)(2,1)} %copy-done.3), custom_call_target="tpu_custom_call" | custom-call | tf_op jit(solution)/shard_map/attn/pallas_call | solution.py:142
  87.8 0.0 copy-done.4
  87.8 0.0 copy-done
  87.8 0.0 copy-start.1
  87.8 1.6 %copy-done.1 = bf16[2048,512]{1,0:T(8,128)(2,1)S(1)} copy-done((bf16[2048,512]{1,0:T(8,128)(2,1)S(1)}, bf16[2048,512]{1,0:T(8,128)(2,1)}, u32[]{:S(2)}) %copy-start.1) | copy-done | bytes 2097176
  89.4 0.0 copy-start.2
  89.4 1.0 copy-done.2
  90.4 19.0 %finish.1 = bf16[512,512]{1,0:T(8,128)(2,1)S(1)} custom-call(bf16[16,32,512]{2,1,0:T(8,128)(2,1)S(1)} %copy-done.2, bf16[16,32,512]{2,1,0:T(8,128)(2,1)S(1)} %get-tuple-element.11.gate_ref, bf16[512,512]{1,0:T(8,128)(2,1)S(1)} %get-tuple-element.12.emb_ref, bf16[512,512]{1,0:T(8,128)(2,1)S(1)} %copy-done.4, bf16[512,2048]{1,0:T(8,128)(2,1)S(1)} %copy-done, ...), custom_call_target="tpu_custom_call" | custom-call | tf_op jit(solution)/shard_map/finish/pallas_call | solution.py:472
  109.4 0.8 copy.11
Async XLA Ops:
  0.0 0.7 copy-start.6
  0.7 0.7 copy-start.7
  1.4 0.7 copy-start.8
  2.0 85.7 %copy-start.4 = (bf16[512,512]{1,0:T(8,128)(2,1)S(1)}, bf16[512,512]{1,0:T(8,128)(2,1)}, u32[]{:S(2)}) copy-start(bf16[512,512]{1,0:T(8,128)(2,1)} %wo_hbm.1) | copy-start | bytes 1572868
  62.4 1.1 %copy-start.3 = (bf16[16,96,512]{2,1,0:T(8,128)(2,1)}, bf16[16,96,512]{2,1,0:T(8,128)(2,1)S(1)}, u32[]{:S(2)}) copy-start(bf16[16,96,512]{2,1,0:T(8,128)(2,1)S(1)} %get-tuple-element.10.qkv_ref) | copy-start | bytes 4718596
  63.6 0.6 copy-start.5
  64.2 23.6 %copy-start = (bf16[512,2048]{1,0:T(8,128)(2,1)S(1)}, bf16[512,2048]{1,0:T(8,128)(2,1)}, u32[]{:S(2)}) copy-start(bf16[512,2048]{1,0:T(8,128)(2,1)} %up_hbm.1) | copy-start | bytes 6291460
  87.8 1.6 %copy-start.1 = (bf16[2048,512]{1,0:T(8,128)(2,1)S(1)}, bf16[2048,512]{1,0:T(8,128)(2,1)}, u32[]{:S(2)}) copy-start(bf16[2048,512]{1,0:T(8,128)(2,1)} %down_hbm.1) | copy-start | bytes 6291460
  89.4 1.0 copy-start.2

commit v3 on v2

v3 whole, which is shorter than its diff:
```python
import functools

import jax
import jax.numpy as jnp
from jax import lax
from jax.experimental import pallas as pl
from jax.experimental.pallas import tpu as pltpu
from jax.sharding import PartitionSpec as P

epsilon = 1e-06

BIG = float(2 ** 30)


def attn_kernel(U, seg_ref, qkv_ref, out_ref, q_scr, k_scr, m_scr, a_scr, acc_scr):
    blocks, _, W = qkv_ref.shape
    bf = jnp.bfloat16
    f32 = jnp.float32
    segments = seg_ref[...]
    s1, s2, s3 = [jnp.sum((segments < s).astype(f32)).astype(jnp.int32) for s in (1, 2, 3)]
    scale = 0.5 / (32.0 ** 0.5)

    def prep(b, carry):
        base = b * W
        lane = lax.broadcasted_iota(jnp.int32, (16, W), 1) + base
        row = lax.broadcasted_iota(jnp.int32, (16, W), 0)
        seg = (lane >= s1).astype(jnp.int32) + (lane >= s2).astype(jnp.int32) + (lane >= s3).astype(jnp.int32)
        same = (seg == row).astype(f32)
        q_scr[b, 0:32] = (qkv_ref[b, 32:64, :].astype(f32) * scale).astype(bf)
        q_scr[b, 32:48] = same.astype(bf)
        bias = jnp.where(row < 4, (1.0 - same) * (-BIG), 0.0).astype(bf)
        k_scr[pl.ds(base, W), :] = jnp.concatenate([qkv_ref[b, 64:96, :], bias], axis=0).T
        return carry

    lax.fori_loop(0, blocks, prep, 0, unroll=2)
    t = lax.broadcasted_iota(jnp.int32, (W, W), 0)
    p = lax.broadcasted_iota(jnp.int32, (W, W), 1)
    m_scr[0] = (t <= p).astype(f32).astype(bf)
    m_scr[1] = jnp.ones((W, W), bf)
    m_scr[2] = jnp.zeros((W, W), bf)

    def low(i):
        first = i * W
        start = jnp.where(first >= s3, s3, jnp.where(first >= s2, s2, jnp.where(first >= s1, s1, 0)))
        return start // W

    total = lax.fori_loop(0, blocks, lambda i, c: c + (i + 1 - low(i)), 0)

    def after(i, j):
        last = j <= low(i)
        return jnp.where(last, i + 1, i), jnp.where(last, i + 1, j - 1)

    def weigh(slot, i, j, valid):
        kind = jnp.where(valid, jnp.where(j == i, 0, 1), 2)
        i = jnp.minimum(i, blocks - 1)
        j = jnp.where(valid, j, 0)
        k = k_scr[pl.ds(pl.multiple_of(j * W, W), W), :]
        s = jnp.dot(k, q_scr[i], preferred_element_type=f32)
        h = s.astype(bf)
        a_scr[slot] = (h + h * jnp.tanh(h)) * m_scr[kind]

    def gather(slot, i, j, valid):
        i = jnp.minimum(i, blocks - 1)
        j = jnp.where(valid, j, 0)
        first = valid & (i == j)
        o = jnp.where(first, 0.0, acc_scr[...])
        o = o + jnp.dot(qkv_ref[j, 0:32, :], a_scr[slot], preferred_element_type=f32)
        acc_scr[...] = o
        out_ref[i] = o.astype(bf)

    def some(n, i, j):
        out = []
        for u in range(U):
            out.append((i, j, n * U + u < total))
            i, j = after(i, j)
        return out, i, j

    zero = jnp.int32(0)
    head, i1, j1 = some(0, zero, zero)
    for u in range(U):
        weigh(u, *head[u])

    def body(n, carry):
        i, j, ni, nj = carry
        now, _, _ = some(n, i, j)
        then, mi, mj = some(n + 1, ni, nj)
        for u in range(U):
            gather(u, *now[u])
            weigh(u, *then[u])
        return ni, nj, mi, mj

    lax.fori_loop(0, (total + U - 1) // U, body, (zero, zero, i1, j1))


def attention(segs, qkv, U):
    blocks, _, W = qkv.shape
    bf = jnp.bfloat16
    vm = pl.BlockSpec(memory_space=pltpu.VMEM)
    return pl.pallas_call(
        functools.partial(attn_kernel, U),
        out_shape=jax.ShapeDtypeStruct((blocks, 32, W), bf),
        in_specs=[vm, vm],
        out_specs=vm,
        scratch_shapes=[
            pltpu.VMEM((blocks, 48, W), bf),
            pltpu.VMEM((blocks * W, 48), bf),
            pltpu.VMEM((3, W, W), bf),
            pltpu.VMEM((U, W, W), bf),
            pltpu.VMEM((32, W), jnp.float32),
        ],
        compiler_params=pltpu.CompilerParams(vmem_limit_bytes=16 << 20),
        name="attn",
    )(segs, qkv)


MESH = pl.DeviceIdType.MESH


def one_hot(ids, base, width):
    lane = lax.broadcasted_iota(jnp.int32, ids.shape, 1).astype(jnp.float32)
    pieces = [
        jnp.where(ids == lane + (base + 128 * c), 1.0, 0.0).astype(jnp.bfloat16) for c in range(width // 128)
    ]
    return jnp.concatenate(pieces, axis=1)


def front_kernel(
    n, m, tok_hbm, seg_hbm, req_hbm, hot_hbm, cold_hbm, w_hbm, emb_ref, gate_ref, recv_ref, segs_ref,
    tok_ref, seg_ref, req_ref, hot, cold, w_ref, x_ref, send, asks, asked, rows_out, rows_in, acc, gat, tokb, idx, flat,
    sends, recvs, msems, lsems,
):
    me_s = lax.axis_index("seq")
    me = lax.axis_index("emb") * n + me_s
    total = n * m
    bf = jnp.bfloat16
    f32 = jnp.float32
    hot_count = hot_hbm.shape[0]
    cold_count = cold_hbm.shape[0]
    hot_rows, cold_rows = 1024, 2048
    side = 4
    me_z, me_y = me_s // side, lax.rem(me_s, side)
    me_x = lax.axis_index("emb") // 2
    far = (2, 1, 3, 0)

    barrier = pltpu.get_barrier_semaphore()

    def device(peer):
        return {"emb": peer // n, "seq": lax.rem(peer, n)}

    def signal(step, carry):
        peer = lax.rem(me + step, total)
        pl.semaphore_signal(barrier, inc=1, device_id=device(peer), device_id_type=MESH)
        return carry

    small = [
        pltpu.make_async_copy(a, b, lsems.at[4 + c])
        for c, (a, b) in enumerate(((tok_hbm, tok_ref), (req_hbm, req_ref), (seg_hbm, seg_ref)))
    ]
    for load in small:
        load.start()
    lax.fori_loop(1, total, signal, 0)
    hot_load = pltpu.make_async_copy(hot_hbm, hot, lsems.at[0])
    cold_load = pltpu.make_async_copy(cold_hbm, cold, lsems.at[1])
    w_load = pltpu.make_async_copy(w_hbm, w_ref, lsems.at[2])
    hot_load.start()
    cold_load.start()
    w_load.start()
    for load in small:
        load.wait()
    wanted = req_ref[0].astype(f32)
    wanted = jnp.concatenate([wanted, jnp.zeros((total - wanted.shape[0], total), f32)], axis=0).T
    asks[...] = wanted.reshape(total, 1, total)
    tokb[...] = jnp.broadcast_to(tok_ref[...].astype(f32), (128, tok_ref.shape[1])).T
    pl.semaphore_wait(barrier, total - 1)

    def ask(peer, src):
        return pltpu.make_async_remote_copy(
            src_ref=asks.at[peer], dst_ref=asked.at[src], send_sem=msems.at[0], recv_sem=msems.at[1],
            device_id=device(peer), device_id_type=MESH,
        )

    def away(step):
        return lax.rem(me_z + 2 + step // side, side) * side + lax.rem(me_y + 2 + step, side)

    def peer_at(dx, core, step):
        return (lax.rem(me_x + dx, side) * 2 + core) * n + away(step)

    def start_ask(step, carry):
        for dx in far:
            for core in range(2):
                peer = peer_at(dx, core, step)

                @pl.when(peer != me)
                def _():
                    ask(peer, me).start()
        return carry

    lax.fori_loop(0, n, start_ask, 0)

    def seg_copy(step, src):
        return pltpu.make_async_remote_copy(
            src_ref=seg_ref, dst_ref=segs_ref.at[src], send_sem=msems.at[4], recv_sem=recvs.at[n + src],
            device_id={"seq": lax.rem(me_s + step, n)}, device_id_type=MESH,
        )

    def start_seg(step, carry):
        seg_copy(step, me_s).start()
        return carry

    lax.fori_loop(1, n, start_seg, 0)
    asked[me] = asks[me]
    segs_ref[me_s] = seg_ref[...]

    hot_load.wait()
    acc[...] = jnp.zeros_like(acc)

    def add_hot(step, carry):
        base = step * hot_rows
        pick = one_hot(tokb[...], base.astype(f32), hot_rows)
        block = hot[pl.ds(pl.multiple_of(base, hot_rows), hot_rows), :]
        acc[...] += jnp.dot(pick, block, preferred_element_type=f32)
        return carry

    lax.fori_loop(0, hot_count // hot_rows, add_hot, 0)

    every = pl.ds(0, total - 1)

    def all_of(src, dst, a, b):
        return pltpu.make_async_remote_copy(
            src_ref=src.at[every], dst_ref=dst.at[every], send_sem=msems.at[a], recv_sem=msems.at[b],
            device_id=device(me), device_id_type=MESH,
        )

    all_of(asks, asked, 0, 1).wait_recv()
    ids = asked[...].reshape(total, 128)
    high = jnp.floor(ids * (1.0 / 64.0))
    low = ids - high * 64.0
    slots = idx.shape[0]
    slot = lax.broadcasted_iota(jnp.int32, (slots, 128), 0)
    lane = lax.broadcasted_iota(jnp.int32, (slots, 128), 1)
    spread = jnp.where(slot // 4 == lane, 1.0, 0.0).astype(bf)
    ids = 64.0 * jnp.dot(spread, high.astype(bf), preferred_element_type=f32) + jnp.dot(
        spread, low.astype(bf), preferred_element_type=f32
    )
    ids = jnp.sum(jnp.where(lax.rem(slot, 4) == lane, ids, 0.0), axis=1, keepdims=True)
    idx[...] = jnp.broadcast_to(ids, (slots, 128))
    cold_load.wait()

    def give(peer, src):
        return pltpu.make_async_remote_copy(
            src_ref=rows_out.at[peer], dst_ref=rows_in.at[src], send_sem=msems.at[2], recv_sem=msems.at[3],
            device_id=device(peer), device_id_type=MESH,
        )

    def serve(first, second):
        gat[...] = jnp.zeros_like(gat)
        group = total // side
        spans = [lax.rem(me_x + dx, side) for dx in (first, second)]
        mine = jnp.concatenate(
            [idx[pl.ds(pl.multiple_of(x * group * 4, group * 4), group * 4), :] for x in spans], axis=0
        )

        def add_cold(step, inner):
            base = step * cold_rows
            pick = one_hot(mine, base.astype(f32), cold_rows)
            block = cold[pl.ds(pl.multiple_of(base, cold_rows), cold_rows), :]
            gat[...] += jnp.dot(pick, block, preferred_element_type=f32)
            return inner

        lax.fori_loop(0, cold_count // cold_rows, add_cold, 0)
        for c, x in enumerate(spans):
            part = gat[c * group * 4:(c + 1) * group * 4, :].astype(bf)
            rows_out[pl.ds(x * group, group)] = part.reshape(group, 4, part.shape[1])

        def start_give(step, inner):
            for dx in (first, second):
                for core in range(2):
                    peer = peer_at(dx, core, step)

                    @pl.when(peer != me)
                    def _():
                        give(peer, me).start()
            return inner

        lax.fori_loop(0, n, start_give, 0)

    serve(2, 1)
    serve(3, 0)
    rows_in[me] = rows_out[me]
    all_of(asks, asked, 0, 1).wait_send()

    all_of(rows_out, rows_in, 2, 3).wait_recv()
    flat[...] = rows_in[...].reshape(flat.shape)
    pick = one_hot(tokb[...], float(hot_count), slots)
    found = (acc[...] + jnp.dot(pick, flat[...], preferred_element_type=f32)).astype(bf)
    emb_ref[...] = found
    x = found.astype(f32)
    x_ref[...] = (x * lax.rsqrt(jnp.mean(x * x, axis=-1, keepdims=True) + epsilon)).astype(bf)
    w_load.wait()

    def copy_to(peer, src):
        return pltpu.make_async_remote_copy(
            src_ref=send.at[peer], dst_ref=recv_ref.at[src], send_sem=sends.at[peer], recv_sem=recvs.at[src],
            device_id={"seq": peer}, device_id_type=MESH,
        )

    for dz in far:
        z = lax.rem(me_z + dz, side)
        block = w_ref[:, pl.ds(pl.multiple_of(z * 512, 512), 512)]
        out = jnp.dot(x_ref[...], block, preferred_element_type=f32).astype(bf).T
        for y in range(side):
            gate_ref[z * side + y] = out[y * 128:y * 128 + 32]
            send[z * side + y] = out[y * 128 + 32:y * 128 + 128]
        for dy in far:
            if (dz, dy) != (0, 0):
                copy_to(z * side + lax.rem(me_y + dy, side), me_s).start()
    recv_ref[me_s] = send[me_s]
    all_of(rows_out, rows_in, 2, 3).wait_send()

    def finish(step, carry):
        source = lax.rem(me_s + n - step, n)
        peer = lax.rem(me_s + step, n)
        copy_to(peer, me_s).wait_send()
        seg_copy(step, source).wait_recv()
        copy_to(peer, source).wait_recv()
        return carry

    lax.fori_loop(1, n, finish, 0)
    pltpu.make_async_remote_copy(
        src_ref=segs_ref.at[pl.ds(0, n - 1)], dst_ref=segs_ref.at[pl.ds(0, n - 1)], send_sem=msems.at[4],
        recv_sem=msems.at[4], device_id=device(me), device_id_type=MESH,
    ).wait_send()


def front(token_rows, segment_ids, requests, hot_table, cold_table, weight, n, m):
    tokens = token_rows.shape[1]
    width = hot_table.shape[1]
    total = n * m
    slots = total * requests.shape[1]
    bf = jnp.bfloat16
    f32 = jnp.float32
    vm = pl.BlockSpec(memory_space=pltpu.VMEM)
    hbm = pl.BlockSpec(memory_space=pltpu.HBM)
    return pl.pallas_call(
        functools.partial(front_kernel, n, m),
        out_shape=(
            jax.ShapeDtypeStruct((tokens, width), bf),
            jax.ShapeDtypeStruct((n, 32, tokens), bf),
            jax.ShapeDtypeStruct((n, 96, tokens), bf),
            jax.ShapeDtypeStruct((n, 1, tokens), jnp.int32),
        ),
        in_specs=[hbm] * 6,
        out_specs=(vm, vm, vm, vm),
        scratch_shapes=[
            pltpu.VMEM(token_rows.shape, jnp.int32),
            pltpu.VMEM(segment_ids.shape, jnp.int32),
            pltpu.VMEM(requests.shape, jnp.int32),
            pltpu.VMEM(hot_table.shape, bf),
            pltpu.VMEM(cold_table.shape, bf),
            pltpu.VMEM(weight.shape, bf),
            pltpu.VMEM((tokens, width), bf),
            pltpu.VMEM((n, 96, tokens), bf),
            pltpu.VMEM((total, 1, 128), f32),
            pltpu.VMEM((total, 1, 128), f32),
            pltpu.VMEM((total, 4, width), bf),
            pltpu.VMEM((total, 4, width), bf),
            pltpu.VMEM((tokens, width), f32),
            pltpu.VMEM((slots // 2, width), f32),
            pltpu.VMEM((tokens, 128), f32),
            pltpu.VMEM((slots, 128), f32),
            pltpu.VMEM((slots, width), bf),
            pltpu.SemaphoreType.DMA((n,)),
            pltpu.SemaphoreType.DMA((2 * n,)),
            pltpu.SemaphoreType.DMA((5,)),
            pltpu.SemaphoreType.DMA((7,)),
        ],
        compiler_params=pltpu.CompilerParams(collective_id=1, has_side_effects=True, vmem_limit_bytes=50 << 20),
        name="front",
    )(*[
        pltpu.with_memory_space_constraint(x, pltpu.HBM)
        for x in (token_rows, segment_ids, requests, hot_table, cold_table, weight)
    ])


def greet(axis_size):
    me = lax.axis_index("seq")
    barrier = pltpu.get_barrier_semaphore()

    def signal(step, carry):
        peer = lax.rem(me + step, axis_size)
        pl.semaphore_signal(barrier, inc=1, device_id={"seq": peer}, device_id_type=MESH)
        return carry

    lax.fori_loop(1, axis_size, signal, 0)
    pl.semaphore_wait(barrier, axis_size - 1)


def finish_kernel(n, att_ref, gate_ref, emb_ref, wo, up, down, out_ref, back, open_gate, sends, recvs):
    me = lax.axis_index("seq")
    greet(n)

    def copy_to(peer, src):
        return pltpu.make_async_remote_copy(
            src_ref=att_ref.at[peer], dst_ref=back.at[src], send_sem=sends.at[peer], recv_sem=recvs.at[src],
            device_id={"seq": peer}, device_id_type=MESH,
        )

    side = 4
    far = (2, 1, 3, 0)
    for dz in far:
        for dy in far:
            if (dz, dy) != (0, 0):
                peer = lax.rem(me // side + dz, side) * side + lax.rem(me + dy, side)
                copy_to(peer, me).start()
    back[me] = att_ref[me]

    def open_one(step, carry):
        gate = gate_ref[step].astype(jnp.float32)
        open_gate[step] = gate / (1.0 + jnp.exp(-gate))
        return carry

    lax.fori_loop(0, n, open_one, 0)

    def finish(step, carry):
        source = lax.rem(me + n - step, n)
        peer = lax.rem(me + step, n)
        copy_to(peer, me).wait_send()
        copy_to(peer, source).wait_recv()
        return carry

    lax.fori_loop(1, n, finish, 0)
    rows = 256

    def tail(step, carry):
        span = pl.ds(pl.multiple_of(step * rows, rows), rows)
        att = back[:, :, span].reshape(n * 32, rows).astype(jnp.float32)
        gate = open_gate[:, :, span].reshape(n * 32, rows)
        scale = lax.rsqrt(jnp.mean(att * att, axis=0, keepdims=True) + epsilon)
        heads = (att * scale * gate).astype(jnp.bfloat16).T
        hidden = emb_ref[span, :].astype(jnp.float32) + jnp.dot(heads, wo[...], preferred_element_type=jnp.float32)
        normed = (hidden * lax.rsqrt(jnp.mean(hidden * hidden, axis=-1, keepdims=True) + epsilon)).astype(jnp.bfloat16)
        wide = jnp.dot(normed, up[...], preferred_element_type=jnp.float32)
        active = (wide / (1.0 + jnp.exp(-wide))).astype(jnp.bfloat16)
        out = hidden + jnp.dot(active, down[...], preferred_element_type=jnp.float32)
        out_ref[span, :] = out.astype(jnp.bfloat16)
        return carry

    lax.fori_loop(0, emb_ref.shape[0] // rows, tail, 0)


def finish_layer(attended, gate, embedded, wo, up, down, n):
    tokens, width = embedded.shape
    bf = jnp.bfloat16
    vm = pl.BlockSpec(memory_space=pltpu.VMEM)
    return pl.pallas_call(
        functools.partial(finish_kernel, n),
        out_shape=jax.ShapeDtypeStruct((tokens, width), bf),
        in_specs=[vm] * 6,
        out_specs=vm,
        scratch_shapes=[
            pltpu.VMEM((n, 32, tokens), bf),
            pltpu.VMEM((n, 32, tokens), jnp.float32),
            pltpu.SemaphoreType.DMA((n,)),
            pltpu.SemaphoreType.DMA((n,)),
        ],
        compiler_params=pltpu.CompilerParams(collective_id=2, has_side_effects=True, vmem_limit_bytes=20 << 20),
        name="finish",
    )(attended, gate, embedded, wo, up, down)


def local(token_rows, segment_ids, requests, hot_table, cold_table, input_weight, output_weight, up_weight, down_weight):
    n = lax.axis_size("seq")
    m = lax.axis_size("emb")
    embedded, gate, triples, segments = front(
        token_rows, segment_ids, jnp.transpose(requests, (0, 2, 1)), hot_table, cold_table, input_weight, n, m
    )
    attended = attention(segments, triples, 4)
    return finish_layer(attended, gate, embedded, output_weight, up_weight, down_weight, n)[None]


def solution(mesh):
    placed = (
        P("emb", "seq"), P("emb", "seq"), P(("emb", "seq"), None, None), P(), P(("emb", "seq"), None), P(), P(), P(), P(),
    )
    return jax.shard_map(local, mesh=mesh, in_specs=placed, out_specs=P("emb", "seq", None), check_vma=False)
```

time: 111 us -> 89.5 us (0.81)
  the two profiles are of different devices: /device:TPU:4 before, /device:TPU:0 now
where the time goes in v3:
time: 89.5 us; the launch traced here: 88.9 us
  Pallas kernels  88.1 us (98%)
    pallas_call x1, Pallas kernels, front(): pl.pallas_call(functools.partial(front_kernel, n, m), out_shape=(jax.Shap...  55.1 us
    pallas_call x1, Pallas kernels, attention(): pl.pallas_call(functools.partial(attn_kernel, U), out_shape=jax.ShapeDtyp...  18.4 us
    pallas_call x1, Pallas kernels, finish_layer(): pl.pallas_call(functools.partial(finish_kernel, n), out_shape=jax.ShapeDt...  14.6 us

profile of v3, /device:TPU:0, one launch (start us, length us, event | category | flops | bytes accessed | tf_op | source)
XLA Modules:
  0.0 88.9 jit_solution(1266648236367089758)
XLA Ops:
  0.0 0.0 copy-start.1
  0.0 0.0 copy-start.2
  0.0 55.1 %front.1 = (bf16[512,512]{1,0:T(8,128)(2,1)S(1)}, bf16[16,32,512]{2,1,0:T(8,128)(2,1)S(1)}, bf16[16,96,512]{2,1,0:T(8,128)(2,1)S(1)}, s32[16,1,512]{2,1,0:T(1,128)S(1)}) custom-call(s32[1,512]{1,0:T(1,128)} %tok_hbm.1, s32[1,512]{1,0:T(1,128)} %seg_hbm.1, s32[1,4,128]{2,1,0:T(4,128)} %bitcast.3, bf16[4096,512]{1,0:T(8,128)(2,1)} %hot_hbm.1, ...), custom_call_target="tpu_custom_call" | custom-call | tf_op jit(solution)/shard_map/front/pallas_call | solution.py:344
  55.1 0.0 copy-start
  55.2 18.4 %attn.1.att_ref = bf16[16,32,512]{2,1,0:T(8,128)(2,1)S(1)} custom-call(s32[16,1,512]{2,1,0:T(1,128)S(1)} %get-tuple-element.9.seg_ref, bf16[16,96,512]{2,1,0:T(8,128)(2,1)S(1)} %get-tuple-element.10.qkv_ref), custom_call_target="tpu_custom_call" | custom-call | tf_op jit(solution)/shard_map/attn/pallas_call | solution.py:99
  73.5 0.0 copy-done.1
  73.5 0.0 copy-done.2
  73.5 0.0 copy-done
  73.5 14.6 %finish.1 = bf16[512,512]{1,0:T(8,128)(2,1)S(1)} custom-call(bf16[16,32,512]{2,1,0:T(8,128)(2,1)S(1)} %attn.1.att_ref, bf16[16,32,512]{2,1,0:T(8,128)(2,1)S(1)} %get-tuple-element.11.gate_ref, bf16[512,512]{1,0:T(8,128)(2,1)S(1)} %get-tuple-element.12.emb_ref, bf16[512,512]{1,0:T(8,128)(2,1)S(1)} %copy-done.2, bf16[512,2048]{1,0:T(8,128)(2,1)S(1)} %copy-done, ...), custom_call_target="tpu_custom_call" | custom-call | tf_op jit(solution)/shard_map/finish/pallas_call | solution.py:455
  88.1 0.8 copy.11
Async XLA Ops:
  0.0 73.5 %copy-start.1 = (bf16[2048,512]{1,0:T(8,128)(2,1)S(1)}, bf16[2048,512]{1,0:T(8,128)(2,1)}, u32[]{:S(2)}) copy-start(bf16[2048,512]{1,0:T(8,128)(2,1)} %down.1) | copy-start | bytes 6291460
  0.0 73.5 %copy-start.2 = (bf16[512,512]{1,0:T(8,128)(2,1)S(1)}, bf16[512,512]{1,0:T(8,128)(2,1)}, u32[]{:S(2)}) copy-start(bf16[512,512]{1,0:T(8,128)(2,1)} %wo.1) | copy-start | bytes 1572868
  55.1 18.4 %copy-start = (bf16[512,2048]{1,0:T(8,128)(2,1)S(1)}, bf16[512,2048]{1,0:T(8,128)(2,1)}, u32[]{:S(2)}) copy-start(bf16[512,2048]{1,0:T(8,128)(2,1)} %up.1) | copy-start | bytes 6291460

commit v4 on v3

--- a/solution.py
+++ b/solution.py
@@ -16,7 +16,7 @@
     blocks, _, W = qkv_ref.shape
     bf = jnp.bfloat16
     f32 = jnp.float32
-    segments = seg_ref[...]
+    segments = seg_ref[:, 0:1, :]
     s1, s2, s3 = [jnp.sum((segments < s).astype(f32)).astype(jnp.int32) for s in (1, 2, 3)]
     scale = 0.5 / (32.0 ** 0.5)
 
@@ -124,53 +124,101 @@
     return jnp.concatenate(pieces, axis=1)
 
 
+def normalize(values):
+    x = values.astype(jnp.float32)
+    return (x * lax.rsqrt(jnp.mean(x * x, axis=-1, keepdims=True) + epsilon)).astype(jnp.bfloat16)
+
+
+def select_exact(pick, ids):
+    high = jnp.floor(ids * (1.0 / 64.0))
+    low = ids - high * 64.0
+    return 64.0 * jnp.dot(pick, high.astype(jnp.bfloat16), preferred_element_type=jnp.float32) + jnp.dot(
+        pick, low.astype(jnp.bfloat16), preferred_element_type=jnp.float32
+    )
+
+
 def front_kernel(
-    n, m, tok_hbm, seg_hbm, req_hbm, hot_hbm, cold_hbm, w_hbm, emb_ref, gate_ref, recv_ref, segs_ref,
-    tok_ref, seg_ref, req_ref, hot, cold, w_ref, x_ref, send, asks, asked, rows_out, rows_in, acc, gat, tokb, idx, flat,
-    sends, recvs, msems, lsems,
+    n, m, tok_hbm, seg_hbm, req_hbm, hot_hbm, cold_hbm, w_hbm, emb_ref, gate_ref, qkv_ref, info_ref,
+    tok_ref, seg_ref, req_ref, hot, cold, w_ref, send, recv, gates, emb_packed, info, asks, asked,
+    rows_out, rows_in, gat, packed, rank_t, idx, flat, msems, crecvs, lsems,
 ):
+    side = 4
     me_s = lax.axis_index("seq")
     me = lax.axis_index("emb") * n + me_s
+    me_z, me_y = me_s // side, lax.rem(me_s, side)
+    me_x = lax.axis_index("emb") // 2
     total = n * m
     bf = jnp.bfloat16
     f32 = jnp.float32
     hot_count = hot_hbm.shape[0]
     cold_count = cold_hbm.shape[0]
-    hot_rows, cold_rows = 1024, 2048
-    side = 4
-    me_z, me_y = me_s // side, lax.rem(me_s, side)
-    me_x = lax.axis_index("emb") // 2
+    tokens = tok_hbm.shape[1]
+    half = tokens // 2
+    slots = idx.shape[0]
     far = (2, 1, 3, 0)
+    wide = 2048
 
     barrier = pltpu.get_barrier_semaphore()
-
-    def device(peer):
-        return {"emb": peer // n, "seq": lax.rem(peer, n)}
-
-    def signal(step, carry):
-        peer = lax.rem(me + step, total)
-        pl.semaphore_signal(barrier, inc=1, device_id=device(peer), device_id_type=MESH)
-        return carry
-
     small = [
-        pltpu.make_async_copy(a, b, lsems.at[4 + c])
+        pltpu.make_async_copy(a, b, lsems.at[3 + c])
         for c, (a, b) in enumerate(((tok_hbm, tok_ref), (req_hbm, req_ref), (seg_hbm, seg_ref)))
     ]
     for load in small:
         load.start()
-    lax.fori_loop(1, total, signal, 0)
+
+    def device(peer):
+        return {"emb": peer // n, "seq": lax.rem(peer, n)}
+
+    def away(step):
+        t = step // side
+        u = lax.rem(step, side)
+        dz = lax.rem(2 + 3 * t + 3 * (t // 2) + 2 * (t // 3), side)
+        dy = lax.rem(2 + 3 * u + 3 * (u // 2) + 2 * (u // 3), side)
+        return dz, dy
+
+    def peer_at(dx, core, step):
+        dz, dy = away(step)
+        return (lax.rem(me_x + dx, side) * 2 + core) * n + lax.rem(me_z + dz, side) * side + lax.rem(me_y + dy, side)
+
+    def signal(step, carry):
+        for dx in far:
+            for core in range(2):
+                peer = peer_at(dx, core, step)
+
+                @pl.when(peer != me)
+                def _():
+                    pl.semaphore_signal(barrier, inc=1, device_id=device(peer), device_id_type=MESH)
+        return carry
+
+    lax.fori_loop(0, n, signal, 0)
     hot_load = pltpu.make_async_copy(hot_hbm, hot, lsems.at[0])
     cold_load = pltpu.make_async_copy(cold_hbm, cold, lsems.at[1])
     w_load = pltpu.make_async_copy(w_hbm, w_ref, lsems.at[2])
     hot_load.start()
+    w_load.start()
     cold_load.start()
-    w_load.start()
     for load in small:
         load.wait()
     wanted = req_ref[0].astype(f32)
     wanted = jnp.concatenate([wanted, jnp.zeros((total - wanted.shape[0], total), f32)], axis=0).T
     asks[...] = wanted.reshape(total, 1, total)
-    tokb[...] = jnp.broadcast_to(tok_ref[...].astype(f32), (128, tok_ref.shape[1])).T
+    tok = tok_ref[...].astype(f32)
+    is_hot = tok < float(hot_count)
+    row = lax.broadcasted_iota(jnp.int32, (tokens, tokens), 0)
+    earlier = row < lax.broadcasted_iota(jnp.int32, (tokens, tokens), 1)
+    marks = jnp.broadcast_to(jnp.where(is_hot, 1.0, 0.0), (8, tokens)).astype(bf)
+    before = jnp.dot(marks, jnp.where(earlier, 1.0, 0.0).astype(bf), preferred_element_type=f32)[0:1]
+    place = lax.broadcasted_iota(jnp.int32, (1, tokens), 1).astype(f32)
+    rank = jnp.where(is_hot, before, half + place - before)
+    info[0:1] = seg_ref[...].astype(f32)
+    info[1:2] = rank
+    rank_t[...] = jnp.broadcast_to(rank, (128, tokens)).T
+
+    def unpacker(ranks, first, count):
+        packed_row = lax.broadcasted_iota(jnp.int32, (count, tokens), 0).astype(f32) + float(first)
+        return jnp.where(packed_row == ranks, 1.0, 0.0).astype(bf)
+
+    packed[...] = select_exact(unpacker(rank, 0, tokens), jnp.broadcast_to(tok, (128, tokens)).T)
     pl.semaphore_wait(barrier, total - 1)
 
     def ask(peer, src):
@@ -179,12 +227,6 @@
             device_id=device(peer), device_id_type=MESH,
         )
 
-    def away(step):
-        return lax.rem(me_z + 2 + step // side, side) * side + lax.rem(me_y + 2 + step, side)
-
-    def peer_at(dx, core, step):
-        return (lax.rem(me_x + dx, side) * 2 + core) * n + away(step)
-
     def start_ask(step, carry):
         for dx in far:
             for core in range(2):
@@ -197,51 +239,76 @@
 
     lax.fori_loop(0, n, start_ask, 0)
 
-    def seg_copy(step, src):
+    def tell(step, carry):
+        pltpu.make_async_remote_copy(
+            src_ref=info, dst_ref=info_ref.at[me_s], send_sem=msems.at[4], recv_sem=msems.at[5],
+            device_id={"seq": lax.rem(me_s + step, n)}, device_id_type=MESH,
+        ).start()
+        return carry
+
+    lax.fori_loop(1, n, tell, 0)
+    asked[me] = asks[me]
+    info_ref[me_s] = info[...]
+
+    def sweep(ids, table, count):
+        gat[...] = jnp.zeros_like(gat)
+
+        def add(step, inner):
+            base = step * wide
+            pick = one_hot(ids, base.astype(f32), wide)
+            block = table[pl.ds(pl.multiple_of(base, wide), wide), :]
+            gat[...] += jnp.dot(pick, block, preferred_element_type=f32)
+            return inner
+
+        lax.fori_loop(0, count // wide, add, 0)
+
+    def part_copy(part, peer, src):
+        span = pl.ds(part * half, half)
         return pltpu.make_async_remote_copy(
-            src_ref=seg_ref, dst_ref=segs_ref.at[src], send_sem=msems.at[4], recv_sem=recvs.at[n + src],
-            device_id={"seq": lax.rem(me_s + step, n)}, device_id_type=MESH,
+            src_ref=send.at[peer, :, span], dst_ref=recv.at[src, :, span], send_sem=msems.at[6 + part],
+            recv_sem=msems.at[8] if part == 0 else crecvs.at[src],
+            device_id={"seq": peer}, device_id_type=MESH,
         )
 
-    def start_seg(step, carry):
-        seg_copy(step, me_s).start()
-        return carry
-
-    lax.fori_loop(1, n, start_seg, 0)
-    asked[me] = asks[me]
-    segs_ref[me_s] = seg_ref[...]
+    def project(part, x):
+        span = slice(part * half, part * half + half)
+        for dz in far:
+            z = lax.rem(me_z + dz, side)
+            block = w_ref[:, pl.ds(pl.multiple_of(z * 512, 512), 512)]
+            out = jnp.dot(x, block, preferred_element_type=f32).astype(bf).T
+            for y in range(side):
+                gates[z * side + y, :, span] = out[y * 128:y * 128 + 32]
+                send[z * side + y, :, span] = out[y * 128 + 32:y * 128 + 128]
+            for dy in far:
+                if (dz, dy) != (0, 0):
+                    part_copy(part, z * side + lax.rem(me_y + dy, side), me_s).start()
+        recv[me_s, :, span] = send[me_s, :, span]
 
     hot_load.wait()
-    acc[...] = jnp.zeros_like(acc)
-
-    def add_hot(step, carry):
-        base = step * hot_rows
-        pick = one_hot(tokb[...], base.astype(f32), hot_rows)
-        block = hot[pl.ds(pl.multiple_of(base, hot_rows), hot_rows), :]
-        acc[...] += jnp.dot(pick, block, preferred_element_type=f32)
-        return carry
-
-    lax.fori_loop(0, hot_count // hot_rows, add_hot, 0)
-
-    every = pl.ds(0, total - 1)
-
-    def all_of(src, dst, a, b):
+    sweep(packed[0:half], hot, hot_count)
+    found = gat[...].astype(bf)
+    emb_packed[0:half] = found
+    w_load.wait()
+    project(0, normalize(found))
+
+    def all_of(src, dst, count, a, b, span=None):
+        every = pl.ds(0, count)
+        src = src.at[every] if span is None else src.at[every, :, span]
+        dst = dst.at[every] if span is None else dst.at[every, :, span]
         return pltpu.make_async_remote_copy(
-            src_ref=src.at[every], dst_ref=dst.at[every], send_sem=msems.at[a], recv_sem=msems.at[b],
+            src_ref=src, dst_ref=dst, send_sem=msems.at[a], recv_sem=msems.at[b],
             device_id=device(me), device_id_type=MESH,
         )
 
-    all_of(asks, asked, 0, 1).wait_recv()
-    ids = asked[...].reshape(total, 128)
-    high = jnp.floor(ids * (1.0 / 64.0))
-    low = ids - high * 64.0
-    slots = idx.shape[0]
+    ask_all = all_of(asks, asked, total - 1, 0, 1)
+    row_all = all_of(rows_out, rows_in, total - 1, 2, 3)
+    info_all = all_of(info_ref, info_ref, n - 1, 4, 5)
+    hot_all = all_of(send, recv, n - 1, 6, 8, pl.ds(0, half))
+    cold_all = all_of(send, recv, n - 1, 7, 8, pl.ds(half, half))
+    ask_all.wait_recv()
     slot = lax.broadcasted_iota(jnp.int32, (slots, 128), 0)
     lane = lax.broadcasted_iota(jnp.int32, (slots, 128), 1)
-    spread = jnp.where(slot // 4 == lane, 1.0, 0.0).astype(bf)
-    ids = 64.0 * jnp.dot(spread, high.astype(bf), preferred_element_type=f32) + jnp.dot(
-        spread, low.astype(bf), preferred_element_type=f32
-    )
+    ids = select_exact(jnp.where(slot // 4 == lane, 1.0, 0.0).astype(bf), asked[...].reshape(total, 128))
     ids = jnp.sum(jnp.where(lax.rem(slot, 4) == lane, ids, 0.0), axis=1, keepdims=True)
     idx[...] = jnp.broadcast_to(ids, (slots, 128))
     cold_load.wait()
@@ -253,21 +320,12 @@
         )
 
     def serve(first, second):
-        gat[...] = jnp.zeros_like(gat)
         group = total // side
         spans = [lax.rem(me_x + dx, side) for dx in (first, second)]
         mine = jnp.concatenate(
             [idx[pl.ds(pl.multiple_of(x * group * 4, group * 4), group * 4), :] for x in spans], axis=0
         )
-
-        def add_cold(step, inner):
-            base = step * cold_rows
-            pick = one_hot(mine, base.astype(f32), cold_rows)
-            block = cold[pl.ds(pl.multiple_of(base, cold_rows), cold_rows), :]
-            gat[...] += jnp.dot(pick, block, preferred_element_type=f32)
-            return inner
-
-        lax.fori_loop(0, cold_count // cold_rows, add_cold, 0)
+        sweep(mine, cold, cold_count)
         for c, x in enumerate(spans):
             part = gat[c * group * 4:(c + 1) * group * 4, :].astype(bf)
             rows_out[pl.ds(x * group, group)] = part.reshape(group, 4, part.shape[1])
@@ -287,49 +345,47 @@
     serve(2, 1)
     serve(3, 0)
     rows_in[me] = rows_out[me]
-    all_of(asks, asked, 0, 1).wait_send()
-
-    all_of(rows_out, rows_in, 2, 3).wait_recv()
+    ask_all.wait_send()
+    info_all.wait_recv()
+    hot_all.wait_recv()
+
+    def unpack_hot(src, carry):
+        pick = unpacker(info_ref[src][1:2], 0, half)
+        qkv_ref[src] = jnp.dot(recv[src, :, 0:half], pick, preferred_element_type=f32).astype(bf)
+        return carry
+
+    lax.fori_loop(0, n, unpack_hot, 0, unroll=2)
+    row_all.wait_recv()
     flat[...] = rows_in[...].reshape(flat.shape)
-    pick = one_hot(tokb[...], float(hot_count), slots)
-    found = (acc[...] + jnp.dot(pick, flat[...], preferred_element_type=f32)).astype(bf)
-    emb_ref[...] = found
-    x = found.astype(f32)
-    x_ref[...] = (x * lax.rsqrt(jnp.mean(x * x, axis=-1, keepdims=True) + epsilon)).astype(bf)
-    w_load.wait()
-
-    def copy_to(peer, src):
-        return pltpu.make_async_remote_copy(
-            src_ref=send.at[peer], dst_ref=recv_ref.at[src], send_sem=sends.at[peer], recv_sem=recvs.at[src],
-            device_id={"seq": peer}, device_id_type=MESH,
-        )
-
-    for dz in far:
-        z = lax.rem(me_z + dz, side)
-        block = w_ref[:, pl.ds(pl.multiple_of(z * 512, 512), 512)]
-        out = jnp.dot(x_ref[...], block, preferred_element_type=f32).astype(bf).T
-        for y in range(side):
-            gate_ref[z * side + y] = out[y * 128:y * 128 + 32]
-            send[z * side + y] = out[y * 128 + 32:y * 128 + 128]
-        for dy in far:
-            if (dz, dy) != (0, 0):
-                copy_to(z * side + lax.rem(me_y + dy, side), me_s).start()
-    recv_ref[me_s] = send[me_s]
-    all_of(rows_out, rows_in, 2, 3).wait_send()
-
-    def finish(step, carry):
-        source = lax.rem(me_s + n - step, n)
-        peer = lax.rem(me_s + step, n)
-        copy_to(peer, me_s).wait_send()
-        seg_copy(step, source).wait_recv()
-        copy_to(peer, source).wait_recv()
-        return carry
-
-    lax.fori_loop(1, n, finish, 0)
-    pltpu.make_async_remote_copy(
-        src_ref=segs_ref.at[pl.ds(0, n - 1)], dst_ref=segs_ref.at[pl.ds(0, n - 1)], send_sem=msems.at[4],
-        recv_sem=msems.at[4], device_id=device(me), device_id_type=MESH,
-    ).wait_send()
+    pick = one_hot(packed[half:tokens], float(hot_count), slots)
+    found = jnp.dot(pick, flat[...], preferred_element_type=f32).astype(bf)
+    emb_packed[half:tokens] = found
+    project(1, normalize(found))
+    pick = one_hot(rank_t[...], 0.0, tokens)
+    emb_ref[...] = jnp.dot(pick, emb_packed[...], preferred_element_type=f32).astype(bf)
+    pick = unpacker(info[1:2], 0, tokens)
+    opened = jnp.dot(gates[...].reshape(tokens, tokens), pick, preferred_element_type=f32).astype(bf)
+    gate_ref[...] = opened.reshape(gate_ref.shape)
+
+    def unpack_cold(src):
+        pick = unpacker(info_ref[src][1:2], half, half)
+        more = jnp.dot(recv[src, :, half:tokens], pick, preferred_element_type=f32)
+        qkv_ref[src] = (qkv_ref[src].astype(f32) + more).astype(bf)
+
+    unpack_cold(me_s)
+
+    def arrive(step, carry):
+        dz, dy = away(step)
+        src = lax.rem(me_z + side - dz, side) * side + lax.rem(me_y + side - dy, side)
+        part_copy(1, src, src).wait_recv()
+        unpack_cold(src)
+        return carry
+
+    lax.fori_loop(0, n - 1, arrive, 0)
+    row_all.wait_send()
+    info_all.wait_send()
+    hot_all.wait_send()
+    cold_all.wait_send()
 
 
 def front(token_rows, segment_ids, requests, hot_table, cold_table, weight, n, m):
@@ -341,13 +397,14 @@
     f32 = jnp.float32
     vm = pl.BlockSpec(memory_space=pltpu.VMEM)
     hbm = pl.BlockSpec(memory_space=pltpu.HBM)
+    operands = (token_rows, segment_ids, requests, hot_table, cold_table, weight)
     return pl.pallas_call(
         functools.partial(front_kernel, n, m),
         out_shape=(
             jax.ShapeDtypeStruct((tokens, width), bf),
             jax.ShapeDtypeStruct((n, 32, tokens), bf),
             jax.ShapeDtypeStruct((n, 96, tokens), bf),
-            jax.ShapeDtypeStruct((n, 1, tokens), jnp.int32),
+            jax.ShapeDtypeStruct((n, 2, tokens), f32),
         ),
         in_specs=[hbm] * 6,
         out_specs=(vm, vm, vm, vm),
@@ -358,28 +415,27 @@
             pltpu.VMEM(hot_table.shape, bf),
             pltpu.VMEM(cold_table.shape, bf),
             pltpu.VMEM(weight.shape, bf),
+            pltpu.VMEM((n, 96, tokens), bf),
+            pltpu.VMEM((n, 96, tokens), bf),
+            pltpu.VMEM((n, 32, tokens), bf),
             pltpu.VMEM((tokens, width), bf),
-            pltpu.VMEM((n, 96, tokens), bf),
+            pltpu.VMEM((2, tokens), f32),
             pltpu.VMEM((total, 1, 128), f32),
             pltpu.VMEM((total, 1, 128), f32),
             pltpu.VMEM((total, 4, width), bf),
             pltpu.VMEM((total, 4, width), bf),
-            pltpu.VMEM((tokens, width), f32),
             pltpu.VMEM((slots // 2, width), f32),
+            pltpu.VMEM((tokens, 128), f32),
             pltpu.VMEM((tokens, 128), f32),
             pltpu.VMEM((slots, 128), f32),
             pltpu.VMEM((slots, width), bf),
+            pltpu.SemaphoreType.DMA((9,)),
             pltpu.SemaphoreType.DMA((n,)),
-            pltpu.SemaphoreType.DMA((2 * n,)),
-            pltpu.SemaphoreType.DMA((5,)),
-            pltpu.SemaphoreType.DMA((7,)),
+            pltpu.SemaphoreType.DMA((6,)),
         ],
-        compiler_params=pltpu.CompilerParams(collective_id=1, has_side_effects=True, vmem_limit_bytes=50 << 20),
+        compiler_params=pltpu.CompilerParams(collective_id=1, has_side_effects=True, vmem_limit_bytes=48 << 20),
         name="front",
-    )(*[
-        pltpu.with_memory_space_constraint(x, pltpu.HBM)
-        for x in (token_rows, segment_ids, requests, hot_table, cold_table, weight)
-    ])
+    )(*[pltpu.with_memory_space_constraint(x, pltpu.HBM) for x in operands])
 
 
 def greet(axis_size):

time: 89.5 us -> 79.7 us (0.89); the launches traced: 88.9 us -> 80.1 us
  Pallas kernels: 88.1 us -> 79.2 us
    pallas_call x1, Pallas kernels: 55.1 us -> 45.8 us  [front(): pl.pallas_call(functools.partial(front_kernel, n, m), out_shape=(jax.Shap...]
where the time goes in v4:
time: 79.7 us; the launch traced here: 80.1 us
  Pallas kernels  79.2 us (99%)
  local copies, waits for them, and re-layouts  0.81 us (1%)
    pallas_call x1, Pallas kernels, front(): pl.pallas_call(functools.partial(front_kernel, n, m), out_shape=(jax.Shap...  45.8 us
    pallas_call x1, Pallas kernels, attention(): pl.pallas_call(functools.partial(attn_kernel, U), out_shape=jax.ShapeDtyp...  18.4 us
    pallas_call x1, Pallas kernels, finish_layer(): pl.pallas_call(functools.partial(finish_kernel, n), out_shape=jax.ShapeDt...  15.1 us

profile of v4, /device:TPU:0, one launch (start us, length us, event | category | flops | bytes accessed | tf_op | source)
XLA Modules:
  0.0 80.1 jit_solution(4938475965068623480)
XLA Ops:
  0.0 0.0 copy-start.1
  0.0 0.0 copy-start.2
  0.0 45.8 %front.1 = (bf16[512,512]{1,0:T(8,128)(2,1)S(1)}, bf16[16,32,512]{2,1,0:T(8,128)(2,1)S(1)}, bf16[16,96,512]{2,1,0:T(8,128)(2,1)S(1)}, f32[16,2,512]{2,1,0:T(2,128)S(1)}) custom-call(s32[1,512]{1,0:T(1,128)} %tok_hbm.1, s32[1,512]{1,0:T(1,128)} %seg_hbm.1, s32[1,4,128]{2,1,0:T(4,128)} %bitcast.3, bf16[4096,512]{1,0:T(8,128)(2,1)} %hot_hbm.1, ...), custom_call_target="tpu_custom_call" | custom-call | tf_op jit(solution)/shard_map/front/pallas_call | solution.py:401
  45.8 0.0 copy-start
  45.8 18.4 %attn.1.att_ref = bf16[16,32,512]{2,1,0:T(8,128)(2,1)S(1)} custom-call(f32[16,2,512]{2,1,0:T(2,128)S(1)} %get-tuple-element.9.seg_ref, bf16[16,96,512]{2,1,0:T(8,128)(2,1)S(1)} %get-tuple-element.10.qkv_ref), custom_call_target="tpu_custom_call" | custom-call | tf_op jit(solution)/shard_map/attn/pallas_call | solution.py:99
  64.2 0.0 copy-done.1
  64.2 0.0 copy-done.2
  64.2 0.0 copy-done
  64.2 15.1 %finish.1 = bf16[512,512]{1,0:T(8,128)(2,1)S(1)} custom-call(bf16[16,32,512]{2,1,0:T(8,128)(2,1)S(1)} %attn.1.att_ref, bf16[16,32,512]{2,1,0:T(8,128)(2,1)S(1)} %get-tuple-element.11.gate_ref, bf16[512,512]{1,0:T(8,128)(2,1)S(1)} %get-tuple-element.12.emb_ref, bf16[512,512]{1,0:T(8,128)(2,1)S(1)} %copy-done.2, bf16[512,2048]{1,0:T(8,128)(2,1)S(1)} %copy-done, ...), custom_call_target="tpu_custom_call" | custom-call | tf_op jit(solution)/shard_map/finish/pallas_call | solution.py:511
  79.3 0.8 copy.11
Async XLA Ops:
  0.0 64.2 %copy-start.1 = (bf16[2048,512]{1,0:T(8,128)(2,1)S(1)}, bf16[2048,512]{1,0:T(8,128)(2,1)}, u32[]{:S(2)}) copy-start(bf16[2048,512]{1,0:T(8,128)(2,1)} %down.1) | copy-start | bytes 6291460
  0.0 64.2 %copy-start.2 = (bf16[512,512]{1,0:T(8,128)(2,1)S(1)}, bf16[512,512]{1,0:T(8,128)(2,1)}, u32[]{:S(2)}) copy-start(bf16[512,512]{1,0:T(8,128)(2,1)} %wo.1) | copy-start | bytes 1572868
  45.8 18.4 %copy-start = (bf16[512,2048]{1,0:T(8,128)(2,1)S(1)}, bf16[512,2048]{1,0:T(8,128)(2,1)}, u32[]{:S(2)}) copy-start(bf16[512,2048]{1,0:T(8,128)(2,1)} %up.1) | copy-start | bytes 6291460

commit v5 on v4

--- a/solution.py
+++ b/solution.py
@@ -12,61 +12,56 @@
 BIG = float(2 ** 30)
 
 
-def attn_kernel(U, seg_ref, qkv_ref, out_ref, q_scr, k_scr, m_scr, a_scr, acc_scr):
-    blocks, _, W = qkv_ref.shape
+def attn_kernel(U, info_ref, q_ref, k_ref, v_ref, out_ref, a_scr, accs):
+    blocks, _, W = q_ref.shape
     bf = jnp.bfloat16
     f32 = jnp.float32
-    segments = seg_ref[:, 0:1, :]
+    half = W // 2
+    segments = info_ref[:, 0:1, :]
     s1, s2, s3 = [jnp.sum((segments < s).astype(f32)).astype(jnp.int32) for s in (1, 2, 3)]
-    scale = 0.5 / (32.0 ** 0.5)
-
-    def prep(b, carry):
-        base = b * W
-        lane = lax.broadcasted_iota(jnp.int32, (16, W), 1) + base
-        row = lax.broadcasted_iota(jnp.int32, (16, W), 0)
-        seg = (lane >= s1).astype(jnp.int32) + (lane >= s2).astype(jnp.int32) + (lane >= s3).astype(jnp.int32)
-        same = (seg == row).astype(f32)
-        q_scr[b, 0:32] = (qkv_ref[b, 32:64, :].astype(f32) * scale).astype(bf)
-        q_scr[b, 32:48] = same.astype(bf)
-        bias = jnp.where(row < 4, (1.0 - same) * (-BIG), 0.0).astype(bf)
-        k_scr[pl.ds(base, W), :] = jnp.concatenate([qkv_ref[b, 64:96, :], bias], axis=0).T
-        return carry
-
-    lax.fori_loop(0, blocks, prep, 0, unroll=2)
-    t = lax.broadcasted_iota(jnp.int32, (W, W), 0)
-    p = lax.broadcasted_iota(jnp.int32, (W, W), 1)
-    m_scr[0] = (t <= p).astype(f32).astype(bf)
-    m_scr[1] = jnp.ones((W, W), bf)
-    m_scr[2] = jnp.zeros((W, W), bf)
+    causal = lax.broadcasted_iota(jnp.int32, (half, half), 0) <= lax.broadcasted_iota(jnp.int32, (half, half), 1)
+
+    def silu(s):
+        h = s.astype(bf)
+        return h + h * jnp.tanh(h)
+
+    def keys(first, count):
+        return k_ref[pl.ds(pl.multiple_of(first, count), count), :]
+
+    def weigh_own(slot, i):
+        q = q_ref[i]
+        early = silu(jnp.dot(keys(i * W, half), q, preferred_element_type=f32))
+        late = silu(jnp.dot(keys(i * W + half, half), q[:, half:], preferred_element_type=f32))
+        zero = jnp.zeros((half, half), bf)
+        a_scr[slot, 0:half, 0:half] = jnp.where(causal, early[:, 0:half], zero)
+        a_scr[slot, 0:half, half:W] = early[:, half:]
+        a_scr[slot, half:W, half:W] = jnp.where(causal, late, zero)
+
+    def gather_own(slot, i):
+        v = v_ref[i]
+        accs[i, :, 0:half] = jnp.dot(v[:, 0:half], a_scr[slot, 0:half, 0:half], preferred_element_type=f32)
+        accs[i, :, half:W] = jnp.dot(v, a_scr[slot, :, half:W], preferred_element_type=f32)
 
     def low(i):
         first = i * W
         start = jnp.where(first >= s3, s3, jnp.where(first >= s2, s2, jnp.where(first >= s1, s1, 0)))
-        return start // W
-
-    total = lax.fori_loop(0, blocks, lambda i, c: c + (i + 1 - low(i)), 0)
+        return jnp.minimum(start // W, i - 1)
+
+    total = lax.fori_loop(1, blocks, lambda i, c: c + (i - low(i)), 0)
 
     def after(i, j):
         last = j <= low(i)
-        return jnp.where(last, i + 1, i), jnp.where(last, i + 1, j - 1)
+        return jnp.where(last, i + 1, i), jnp.where(last, i, j - 1)
 
     def weigh(slot, i, j, valid):
-        kind = jnp.where(valid, jnp.where(j == i, 0, 1), 2)
-        i = jnp.minimum(i, blocks - 1)
+        i = jnp.where(valid, i, 0)
         j = jnp.where(valid, j, 0)
-        k = k_scr[pl.ds(pl.multiple_of(j * W, W), W), :]
-        s = jnp.dot(k, q_scr[i], preferred_element_type=f32)
-        h = s.astype(bf)
-        a_scr[slot] = (h + h * jnp.tanh(h)) * m_scr[kind]
+        a_scr[slot] = silu(jnp.dot(keys(j * W, W), q_ref[i], preferred_element_type=f32))
 
     def gather(slot, i, j, valid):
-        i = jnp.minimum(i, blocks - 1)
+        i = jnp.where(valid, i, blocks)
         j = jnp.where(valid, j, 0)
-        first = valid & (i == j)
-        o = jnp.where(first, 0.0, acc_scr[...])
-        o = o + jnp.dot(qkv_ref[j, 0:32, :], a_scr[slot], preferred_element_type=f32)
-        acc_scr[...] = o
-        out_ref[i] = o.astype(bf)
+        accs[i] = accs[i] + jnp.dot(v_ref[j], a_scr[slot], preferred_element_type=f32)
 
     def some(n, i, j):
         out = []
@@ -75,9 +70,21 @@
             i, j = after(i, j)
         return out, i, j
 
-    zero = jnp.int32(0)
-    head, i1, j1 = some(0, zero, zero)
+    accs[blocks] = jnp.zeros(accs.shape[1:], f32)
     for u in range(U):
+        weigh_own(u, u)
+
+    def own_body(g, carry):
+        for u in range(U):
+            gather_own(u, g * U + u)
+            weigh_own(u, (g + 1) * U + u)
+        return carry
+
+    lax.fori_loop(0, blocks // U - 1, own_body, 0)
+    one, zero = jnp.int32(1), jnp.int32(0)
+    head, i1, j1 = some(0, one, zero)
+    for u in range(U):
+        gather_own(u, blocks - U + u)
         weigh(u, *head[u])
 
     def body(n, carry):
@@ -89,28 +96,24 @@
             weigh(u, *then[u])
         return ni, nj, mi, mj
 
-    lax.fori_loop(0, (total + U - 1) // U, body, (zero, zero, i1, j1))
-
-
-def attention(segs, qkv, U):
-    blocks, _, W = qkv.shape
+    lax.fori_loop(0, (total + U - 1) // U, body, (one, zero, i1, j1))
+    for i in range(blocks):
+        out_ref[i] = accs[i].astype(bf)
+
+
+def attention(info, q, k, v, U):
+    blocks, _, W = q.shape
     bf = jnp.bfloat16
     vm = pl.BlockSpec(memory_space=pltpu.VMEM)
     return pl.pallas_call(
         functools.partial(attn_kernel, U),
         out_shape=jax.ShapeDtypeStruct((blocks, 32, W), bf),
-        in_specs=[vm, vm],
+        in_specs=[vm] * 4,
         out_specs=vm,
-        scratch_shapes=[
-            pltpu.VMEM((blocks, 48, W), bf),
-            pltpu.VMEM((blocks * W, 48), bf),
-            pltpu.VMEM((3, W, W), bf),
-            pltpu.VMEM((U, W, W), bf),
-            pltpu.VMEM((32, W), jnp.float32),
-        ],
+        scratch_shapes=[pltpu.VMEM((U, W, W), bf), pltpu.VMEM((blocks + 1, 32, W), jnp.float32)],
         compiler_params=pltpu.CompilerParams(vmem_limit_bytes=16 << 20),
         name="attn",
-    )(segs, qkv)
+    )(info, q, k, v)
 
 
 MESH = pl.DeviceIdType.MESH
@@ -138,8 +141,8 @@
 
 
 def front_kernel(
-    n, m, tok_hbm, seg_hbm, req_hbm, hot_hbm, cold_hbm, w_hbm, emb_ref, gate_ref, qkv_ref, info_ref,
-    tok_ref, seg_ref, req_ref, hot, cold, w_ref, send, recv, gates, emb_packed, info, asks, asked,
+    n, m, tok_hbm, seg_hbm, req_hbm, hot_hbm, cold_hbm, w_hbm, emb_ref, gate_ref, q_ref, k_ref, v_ref, info_ref,
+    part, tok_ref, seg_ref, req_ref, hot, cold, w_ref, send, recv, gates, emb_packed, info, asks, asked,
     rows_out, rows_in, gat, packed, rank_t, idx, flat, msems, crecvs, lsems,
 ):
     side = 4
@@ -157,6 +160,7 @@
     slots = idx.shape[0]
     far = (2, 1, 3, 0)
     wide = 2048
+    scale = 0.5 / (32.0 ** 0.5)
 
     barrier = pltpu.get_barrier_semaphore()
     small = [
@@ -262,16 +266,16 @@
 
         lax.fori_loop(0, count // wide, add, 0)
 
-    def part_copy(part, peer, src):
-        span = pl.ds(part * half, half)
+    def part_copy(piece, peer, src):
+        span = pl.ds(piece * half, half)
         return pltpu.make_async_remote_copy(
-            src_ref=send.at[peer, :, span], dst_ref=recv.at[src, :, span], send_sem=msems.at[6 + part],
-            recv_sem=msems.at[8] if part == 0 else crecvs.at[src],
+            src_ref=send.at[peer, :, span], dst_ref=recv.at[src, :, span], send_sem=msems.at[6 + piece],
+            recv_sem=msems.at[8] if piece == 0 else crecvs.at[src],
             device_id={"seq": peer}, device_id_type=MESH,
         )
 
-    def project(part, x):
-        span = slice(part * half, part * half + half)
+    def project(piece, x):
+        span = slice(piece * half, piece * half + half)
         for dz in far:
             z = lax.rem(me_z + dz, side)
             block = w_ref[:, pl.ds(pl.multiple_of(z * 512, 512), 512)]
@@ -281,7 +285,7 @@
                 send[z * side + y, :, span] = out[y * 128 + 32:y * 128 + 128]
             for dy in far:
                 if (dz, dy) != (0, 0):
-                    part_copy(part, z * side + lax.rem(me_y + dy, side), me_s).start()
+                    part_copy(piece, z * side + lax.rem(me_y + dy, side), me_s).start()
         recv[me_s, :, span] = send[me_s, :, span]
 
     hot_load.wait()
@@ -327,8 +331,8 @@
         )
         sweep(mine, cold, cold_count)
         for c, x in enumerate(spans):
-            part = gat[c * group * 4:(c + 1) * group * 4, :].astype(bf)
-            rows_out[pl.ds(x * group, group)] = part.reshape(group, 4, part.shape[1])
+            share = gat[c * group * 4:(c + 1) * group * 4, :].astype(bf)
+            rows_out[pl.ds(x * group, group)] = share.reshape(group, 4, share.shape[1])
 
         def start_give(step, inner):
             for dx in (first, second):
@@ -351,7 +355,7 @@
 
     def unpack_hot(src, carry):
         pick = unpacker(info_ref[src][1:2], 0, half)
-        qkv_ref[src] = jnp.dot(recv[src, :, 0:half], pick, preferred_element_type=f32).astype(bf)
+        part[src] = jnp.dot(recv[src, :, 0:half], pick, preferred_element_type=f32).astype(bf)
         return carry
 
     lax.fori_loop(0, n, unpack_hot, 0, unroll=2)
@@ -370,7 +374,15 @@
     def unpack_cold(src):
         pick = unpacker(info_ref[src][1:2], half, half)
         more = jnp.dot(recv[src, :, half:tokens], pick, preferred_element_type=f32)
-        qkv_ref[src] = (qkv_ref[src].astype(f32) + more).astype(bf)
+        whole = part[src].astype(f32) + more
+        v_ref[src] = whole[0:32].astype(bf)
+        q_ref[src, 0:32] = (whole[32:64] * scale).astype(bf)
+        row = lax.broadcasted_iota(jnp.int32, (16, tokens), 0).astype(f32)
+        same = jnp.where(info_ref[src][0:1] == row, 1.0, 0.0)
+        q_ref[src, 32:48] = same.astype(bf)
+        bias = jnp.where(row < 4.0, (1.0 - same) * (-BIG), 0.0)
+        extended = jnp.concatenate([whole[64:96], bias], axis=0).astype(bf)
+        k_ref[pl.ds(pl.multiple_of(src * tokens, tokens), tokens), :] = extended.T
 
     unpack_cold(me_s)
 
@@ -403,12 +415,15 @@
         out_shape=(
             jax.ShapeDtypeStruct((tokens, width), bf),
             jax.ShapeDtypeStruct((n, 32, tokens), bf),
-            jax.ShapeDtypeStruct((n, 96, tokens), bf),
+            jax.ShapeDtypeStruct((n, 48, tokens), bf),
+            jax.ShapeDtypeStruct((n * tokens, 48), bf),
+            jax.ShapeDtypeStruct((n, 32, tokens), bf),
             jax.ShapeDtypeStruct((n, 2, tokens), f32),
         ),
         in_specs=[hbm] * 6,
-        out_specs=(vm, vm, vm, vm),
+        out_specs=(vm,) * 6,
         scratch_shapes=[
+            pltpu.VMEM((n, 96, tokens), bf),
             pltpu.VMEM(token_rows.shape, jnp.int32),
             pltpu.VMEM(segment_ids.shape, jnp.int32),
             pltpu.VMEM(requests.shape, jnp.int32),
@@ -433,7 +448,7 @@
             pltpu.SemaphoreType.DMA((n,)),
             pltpu.SemaphoreType.DMA((6,)),
         ],
-        compiler_params=pltpu.CompilerParams(collective_id=1, has_side_effects=True, vmem_limit_bytes=48 << 20),
+        compiler_params=pltpu.CompilerParams(collective_id=1, has_side_effects=True, vmem_limit_bytes=46 << 20),
         name="front",
     )(*[pltpu.with_memory_space_constraint(x, pltpu.HBM) for x in operands])
 
@@ -455,20 +470,24 @@
     me = lax.axis_index("seq")
     greet(n)
 
-    def copy_to(peer, src):
+    tokens = emb_ref.shape[0]
+    rows = tokens // 2
+
+    def copy_to(part, peer):
         return pltpu.make_async_remote_copy(
-            src_ref=att_ref.at[peer], dst_ref=back.at[src], send_sem=sends.at[peer], recv_sem=recvs.at[src],
-            device_id={"seq": peer}, device_id_type=MESH,
+            src_ref=att_ref.at[peer, :, pl.ds(part * rows, rows)], dst_ref=back.at[part, me], send_sem=sends,
+            recv_sem=recvs.at[part], device_id={"seq": peer}, device_id_type=MESH,
         )
 
     side = 4
     far = (2, 1, 3, 0)
-    for dz in far:
-        for dy in far:
-            if (dz, dy) != (0, 0):
-                peer = lax.rem(me // side + dz, side) * side + lax.rem(me + dy, side)
-                copy_to(peer, me).start()
-    back[me] = att_ref[me]
+    for part in range(2):
+        for dz in far:
+            for dy in far:
+                if (dz, dy) != (0, 0):
+                    copy_to(part, lax.rem(me // side + dz, side) * side + lax.rem(me + dy, side)).start()
+    for part in range(2):
+        back[part, me] = att_ref[me, :, part * rows:(part + 1) * rows]
 
     def open_one(step, carry):
         gate = gate_ref[step].astype(jnp.float32)
@@ -477,19 +496,15 @@
 
     lax.fori_loop(0, n, open_one, 0)
 
-    def finish(step, carry):
-        source = lax.rem(me + n - step, n)
-        peer = lax.rem(me + step, n)
-        copy_to(peer, me).wait_send()
-        copy_to(peer, source).wait_recv()
-        return carry
-
-    lax.fori_loop(1, n, finish, 0)
-    rows = 256
-
-    def tail(step, carry):
-        span = pl.ds(pl.multiple_of(step * rows, rows), rows)
-        att = back[:, :, span].reshape(n * 32, rows).astype(jnp.float32)
+    every = pl.ds(0, n - 1)
+
+    def tail(step):
+        span = slice(step * rows, (step + 1) * rows)
+        pltpu.make_async_remote_copy(
+            src_ref=back.at[step, every], dst_ref=back.at[step, every], send_sem=sends, recv_sem=recvs.at[step],
+            device_id={"seq": me}, device_id_type=MESH,
+        ).wait_recv()
+        att = back[step].reshape(n * 32, rows).astype(jnp.float32)
         gate = open_gate[:, :, span].reshape(n * 32, rows)
         scale = lax.rsqrt(jnp.mean(att * att, axis=0, keepdims=True) + epsilon)
         heads = (att * scale * gate).astype(jnp.bfloat16).T
@@ -499,9 +514,13 @@
         active = (wide / (1.0 + jnp.exp(-wide))).astype(jnp.bfloat16)
         out = hidden + jnp.dot(active, down[...], preferred_element_type=jnp.float32)
         out_ref[span, :] = out.astype(jnp.bfloat16)
-        return carry
-
-    lax.fori_loop(0, emb_ref.shape[0] // rows, tail, 0)
+
+    for step in range(2):
+        tail(step)
+    pltpu.make_async_remote_copy(
+        src_ref=att_ref.at[every], dst_ref=att_ref.at[every], send_sem=sends, recv_sem=recvs.at[0],
+        device_id={"seq": me}, device_id_type=MESH,
+    ).wait_send()
 
 
 def finish_layer(attended, gate, embedded, wo, up, down, n):
@@ -514,10 +533,10 @@
         in_specs=[vm] * 6,
         out_specs=vm,
         scratch_shapes=[
-            pltpu.VMEM((n, 32, tokens), bf),
+            pltpu.VMEM((2, n, 32, tokens // 2), bf),
             pltpu.VMEM((n, 32, tokens), jnp.float32),
-            pltpu.SemaphoreType.DMA((n,)),
-            pltpu.SemaphoreType.DMA((n,)),
+            pltpu.SemaphoreType.DMA,
+            pltpu.SemaphoreType.DMA((2,)),
         ],
         compiler_params=pltpu.CompilerParams(collective_id=2, has_side_effects=True, vmem_limit_bytes=20 << 20),
         name="finish",
@@ -527,10 +546,10 @@
 def local(token_rows, segment_ids, requests, hot_table, cold_table, input_weight, output_weight, up_weight, down_weight):
     n = lax.axis_size("seq")
     m = lax.axis_size("emb")
-    embedded, gate, triples, segments = front(
+    embedded, gate, q, k, v, info = front(
         token_rows, segment_ids, jnp.transpose(requests, (0, 2, 1)), hot_table, cold_table, input_weight, n, m
     )
-    attended = attention(segments, triples, 4)
+    attended = attention(info, q, k, v, 8)
     return finish_layer(attended, gate, embedded, output_weight, up_weight, down_weight, n)[None]
 
 

time: 79.7 us -> 77.5 us (0.972); the launches traced: 80.1 us -> 77 us
  Pallas kernels: 79.2 us -> 76.1 us
    pallas_call x1, Pallas kernels: 15.1 us -> 12.2 us  [finish_layer(): pl.pallas_call(functools.partial(finish_kernel, n), out_shape=jax.ShapeDt...]
    pallas_call x1, Pallas kernels: 18.4 us -> 17.1 us  [attention(): pl.pallas_call(functools.partial(attn_kernel, U), out_shape=jax.ShapeDtyp...]
    pallas_call x1, Pallas kernels: 45.8 us -> 46.7 us  [front(): pl.pallas_call(functools.partial(front_kernel, n, m), out_shape=(jax.Shap...]
where the time goes in v5:
time: 77.5 us; the launch traced here: 77 us
  Pallas kernels  76.1 us (98%)
  local copies, waits for them, and re-layouts  0.81 us (1%)
    pallas_call x1, Pallas kernels, front(): pl.pallas_call(functools.partial(front_kernel, n, m), out_shape=(jax.Shap...  46.7 us
    pallas_call x1, Pallas kernels, attention(): pl.pallas_call(functools.partial(attn_kernel, U), out_shape=jax.ShapeDtyp...  17.1 us
    pallas_call x1, Pallas kernels, finish_layer(): pl.pallas_call(functools.partial(finish_kernel, n), out_shape=jax.ShapeDt...  12.2 us

profile of v5, /device:TPU:0, one launch (start us, length us, event | category | flops | bytes accessed | tf_op | source)
XLA Modules:
  0.0 77.0 jit_solution(60160770640435116)
XLA Ops:
  0.0 0.0 copy-start.1
  0.0 46.7 %front.1 = (bf16[512,512]{1,0:T(8,128)(2,1)S(1)}, bf16[16,32,512]{2,1,0:T(8,128)(2,1)S(1)}, bf16[16,48,512]{2,1,0:T(8,128)(2,1)S(1)}, bf16[8192,48]{1,0:T(8,128)...) custom-call(s32[1,512]{1,0:T(1,128)} %tok_hbm.1, s32[1,512]{1,0:T(1,128)} %seg_hbm.1, ...), custom_call_target="tpu_custom_call" | custom-call | tf_op jit(solution)/shard_map/front/pallas_call | solution.py:413
  46.7 0.0 copy-start
  46.7 0.0 copy-start.2
  46.8 17.1 %attn.1.att_ref = bf16[16,32,512]{2,1,0:T(8,128)(2,1)S(1)} custom-call(f32[16,2,512]{2,1,0:T(2,128)S(1)} %get-tuple-element.11.info_ref, bf16[16,48,512]{2,1,0:T(8,128)(2,1)S(1)} %get-tuple-element.12.q_ref, bf16[8192,48]{1,0:T(8,128)(2,1)S(1)} %get-tuple-element.13.k_ref, bf16[16,32,512]{2,1,0:T(8,128)(2,1)S(1)} %get-tuple-element.14.v_ref), custom_call_target="tpu_custom_call" | custom-call | tf_op jit(solution)/shard_map/attn/pallas_call | solution.py:108
  63.9 0.0 copy-done.1
  63.9 0.0 copy-done
  63.9 0.0 copy-done.2
  63.9 12.2 %finish.1 = bf16[512,512]{1,0:T(8,128)(2,1)S(1)} custom-call(bf16[16,32,512]{2,1,0:T(8,128)(2,1)S(1)} %attn.1.att_ref, bf16[16,32,512]{2,1,0:T(8,128)(2,1)S(1)} %get-tuple-element.15.gate_ref, bf16[512,512]{1,0:T(8,128)(2,1)S(1)} %get-tuple-element.16.emb_ref, bf16[512,512]{1,0:T(8,128)(2,1)S(1)} %copy-done.2, bf16[512,2048]{1,0:T(8,128)(2,1)S(1)} %copy-done, ...), custom_call_target="tpu_custom_call" | custom-call | tf_op jit(solution)/shard_map/finish/pallas_call | solution.py:530
  76.2 0.8 %copy.11 = bf16[1,512,512]{2,1,0:T(8,128)(2,1)} copy(bf16[1,512,512]{2,1,0:T(8,128)(2,1)S(1)} %bitcast.2) | data formatting | bytes 1048576
Async XLA Ops:
  0.0 63.9 %copy-start.1 = (bf16[2048,512]{1,0:T(8,128)(2,1)S(1)}, bf16[2048,512]{1,0:T(8,128)(2,1)}, u32[]{:S(2)}) copy-start(bf16[2048,512]{1,0:T(8,128)(2,1)} %down.1) | copy-start | bytes 6291460
  46.7 17.2 %copy-start = (bf16[512,2048]{1,0:T(8,128)(2,1)S(1)}, bf16[512,2048]{1,0:T(8,128)(2,1)}, u32[]{:S(2)}) copy-start(bf16[512,2048]{1,0:T(8,128)(2,1)} %up.1) | copy-start | bytes 6291460
  46.7 17.2 %copy-start.2 = (bf16[512,512]{1,0:T(8,128)(2,1)S(1)}, bf16[512,512]{1,0:T(8,128)(2,1)}, u32[]{:S(2)}) copy-start(bf16[512,512]{1,0:T(8,128)(2,1)} %wo.1) | copy-start | bytes 1572868

commit v6 on v5

--- a/solution.py
+++ b/solution.py
@@ -12,56 +12,44 @@
 BIG = float(2 ** 30)
 
 
-def attn_kernel(U, info_ref, q_ref, k_ref, v_ref, out_ref, a_scr, accs):
+def silu_half(s):
+    h = s.astype(jnp.bfloat16)
+    return h + h * jnp.tanh(h)
+
+
+def attn_kernel(U, info_ref, q_ref, k_ref, v_ref, own_ref, out_ref, a_scr, accs):
     blocks, _, W = q_ref.shape
     bf = jnp.bfloat16
     f32 = jnp.float32
     half = W // 2
     segments = info_ref[:, 0:1, :]
     s1, s2, s3 = [jnp.sum((segments < s).astype(f32)).astype(jnp.int32) for s in (1, 2, 3)]
-    causal = lax.broadcasted_iota(jnp.int32, (half, half), 0) <= lax.broadcasted_iota(jnp.int32, (half, half), 1)
-
-    def silu(s):
-        h = s.astype(bf)
-        return h + h * jnp.tanh(h)
-
-    def keys(first, count):
-        return k_ref[pl.ds(pl.multiple_of(first, count), count), :]
-
-    def weigh_own(slot, i):
-        q = q_ref[i]
-        early = silu(jnp.dot(keys(i * W, half), q, preferred_element_type=f32))
-        late = silu(jnp.dot(keys(i * W + half, half), q[:, half:], preferred_element_type=f32))
-        zero = jnp.zeros((half, half), bf)
-        a_scr[slot, 0:half, 0:half] = jnp.where(causal, early[:, 0:half], zero)
-        a_scr[slot, 0:half, half:W] = early[:, half:]
-        a_scr[slot, half:W, half:W] = jnp.where(causal, late, zero)
-
-    def gather_own(slot, i):
-        v = v_ref[i]
-        accs[i, :, 0:half] = jnp.dot(v[:, 0:half], a_scr[slot, 0:half, 0:half], preferred_element_type=f32)
-        accs[i, :, half:W] = jnp.dot(v, a_scr[slot, :, half:W], preferred_element_type=f32)
+    for i in range(blocks):
+        accs[i] = own_ref[i]
+    accs[blocks] = jnp.zeros(accs.shape[1:], f32)
 
     def low(i):
         first = i * W
         start = jnp.where(first >= s3, s3, jnp.where(first >= s2, s2, jnp.where(first >= s1, s1, 0)))
-        return jnp.minimum(start // W, i - 1)
-
-    total = lax.fori_loop(1, blocks, lambda i, c: c + (i - low(i)), 0)
+        return jnp.minimum(start // half, 2 * i - 1)
+
+    total = lax.fori_loop(1, blocks, lambda i, c: c + (2 * i - low(i)), 0)
 
     def after(i, j):
         last = j <= low(i)
-        return jnp.where(last, i + 1, i), jnp.where(last, i, j - 1)
+        return jnp.where(last, i + 1, i), jnp.where(last, 2 * i + 1, j - 1)
 
     def weigh(slot, i, j, valid):
         i = jnp.where(valid, i, 0)
         j = jnp.where(valid, j, 0)
-        a_scr[slot] = silu(jnp.dot(keys(j * W, W), q_ref[i], preferred_element_type=f32))
+        keys = k_ref[pl.ds(pl.multiple_of(j * half, half), half), :]
+        a_scr[slot] = silu_half(jnp.dot(keys, q_ref[i], preferred_element_type=f32))
 
     def gather(slot, i, j, valid):
         i = jnp.where(valid, i, blocks)
         j = jnp.where(valid, j, 0)
-        accs[i] = accs[i] + jnp.dot(v_ref[j], a_scr[slot], preferred_element_type=f32)
+        values = v_ref[j // 2, :, pl.ds(pl.multiple_of(lax.rem(j, 2) * half, half), half)]
+        accs[i] = accs[i] + jnp.dot(values, a_scr[slot], preferred_element_type=f32)
 
     def some(n, i, j):
         out = []
@@ -70,21 +58,9 @@
             i, j = after(i, j)
         return out, i, j
 
-    accs[blocks] = jnp.zeros(accs.shape[1:], f32)
+    one = jnp.int32(1)
+    head, i1, j1 = some(0, one, one)
     for u in range(U):
-        weigh_own(u, u)
-
-    def own_body(g, carry):
-        for u in range(U):
-            gather_own(u, g * U + u)
-            weigh_own(u, (g + 1) * U + u)
-        return carry
-
-    lax.fori_loop(0, blocks // U - 1, own_body, 0)
-    one, zero = jnp.int32(1), jnp.int32(0)
-    head, i1, j1 = some(0, one, zero)
-    for u in range(U):
-        gather_own(u, blocks - U + u)
         weigh(u, *head[u])
 
     def body(n, carry):
@@ -96,24 +72,24 @@
             weigh(u, *then[u])
         return ni, nj, mi, mj
 
-    lax.fori_loop(0, (total + U - 1) // U, body, (one, zero, i1, j1))
+    lax.fori_loop(0, (total + U - 1) // U, body, (one, one, i1, j1))
     for i in range(blocks):
         out_ref[i] = accs[i].astype(bf)
 
 
-def attention(info, q, k, v, U):
+def attention(info, q, k, v, own, U):
     blocks, _, W = q.shape
     bf = jnp.bfloat16
     vm = pl.BlockSpec(memory_space=pltpu.VMEM)
     return pl.pallas_call(
         functools.partial(attn_kernel, U),
         out_shape=jax.ShapeDtypeStruct((blocks, 32, W), bf),
-        in_specs=[vm] * 4,
+        in_specs=[vm] * 5,
         out_specs=vm,
-        scratch_shapes=[pltpu.VMEM((U, W, W), bf), pltpu.VMEM((blocks + 1, 32, W), jnp.float32)],
-        compiler_params=pltpu.CompilerParams(vmem_limit_bytes=16 << 20),
+        scratch_shapes=[pltpu.VMEM((U, W // 2, W), bf), pltpu.VMEM((blocks + 1, 32, W), jnp.float32)],
+        compiler_params=pltpu.CompilerParams(vmem_limit_bytes=18 << 20),
         name="attn",
-    )(info, q, k, v)
+    )(info, q, k, v, own)
 
 
 MESH = pl.DeviceIdType.MESH
@@ -141,8 +117,8 @@
 
 
 def front_kernel(
-    n, m, tok_hbm, seg_hbm, req_hbm, hot_hbm, cold_hbm, w_hbm, emb_ref, gate_ref, q_ref, k_ref, v_ref, info_ref,
-    part, tok_ref, seg_ref, req_ref, hot, cold, w_ref, send, recv, gates, emb_packed, info, asks, asked,
+    n, m, tok_hbm, seg_hbm, req_hbm, hot_hbm, cold_hbm, w_hbm, emb_ref, gate_ref, q_ref, k_ref, v_ref, info_ref, own_ref,
+    weights, part, tok_ref, seg_ref, req_ref, hot, cold, w_ref, send, recv, gates, emb_packed, info, asks, asked,
     rows_out, rows_in, gat, packed, rank_t, idx, flat, msems, crecvs, lsems,
 ):
     side = 4
@@ -159,7 +135,7 @@
     half = tokens // 2
     slots = idx.shape[0]
     far = (2, 1, 3, 0)
-    wide = 2048
+    wide = 4096
     scale = 0.5 / (32.0 ** 0.5)
 
     barrier = pltpu.get_barrier_semaphore()
@@ -384,16 +360,34 @@
         extended = jnp.concatenate([whole[64:96], bias], axis=0).astype(bf)
         k_ref[pl.ds(pl.multiple_of(src * tokens, tokens), tokens), :] = extended.T
 
+    causal = lax.broadcasted_iota(jnp.int32, (half, half), 0) <= lax.broadcasted_iota(jnp.int32, (half, half), 1)
+
+    def attend_own(src):
+        q = q_ref[src]
+        v = v_ref[src]
+        first = pl.multiple_of(src * tokens, tokens)
+        early = k_ref[pl.ds(first, half), :]
+        late = k_ref[pl.ds(pl.multiple_of(first + half, half), half), :]
+        early = silu_half(jnp.dot(early, q, preferred_element_type=f32))
+        late = silu_half(jnp.dot(late, q[:, half:], preferred_element_type=f32))
+        zero = jnp.zeros((half, half), bf)
+        weights[0:half, 0:half] = jnp.where(causal, early[:, 0:half], zero)
+        weights[0:half, half:] = early[:, half:]
+        weights[half:, half:] = jnp.where(causal, late, zero)
+        own_ref[src, :, 0:half] = jnp.dot(v[:, 0:half], weights[0:half, 0:half], preferred_element_type=f32)
+        own_ref[src, :, half:] = jnp.dot(v, weights[:, half:], preferred_element_type=f32)
+
     unpack_cold(me_s)
 
-    def arrive(step, carry):
+    def arrive(step, before):
         dz, dy = away(step)
         src = lax.rem(me_z + side - dz, side) * side + lax.rem(me_y + side - dy, side)
         part_copy(1, src, src).wait_recv()
+        attend_own(before)
         unpack_cold(src)
-        return carry
-
-    lax.fori_loop(0, n - 1, arrive, 0)
+        return src
+
+    attend_own(lax.fori_loop(0, n - 1, arrive, me_s))
     row_all.wait_send()
     info_all.wait_send()
     hot_all.wait_send()
@@ -419,10 +413,12 @@
             jax.ShapeDtypeStruct((n * tokens, 48), bf),
             jax.ShapeDtypeStruct((n, 32, tokens), bf),
             jax.ShapeDtypeStruct((n, 2, tokens), f32),
+            jax.ShapeDtypeStruct((n, 32, tokens), f32),
         ),
         in_specs=[hbm] * 6,
-        out_specs=(vm,) * 6,
+        out_specs=(vm,) * 7,
         scratch_shapes=[
+            pltpu.VMEM((tokens, tokens), bf),
             pltpu.VMEM((n, 96, tokens), bf),
             pltpu.VMEM(token_rows.shape, jnp.int32),
             pltpu.VMEM(segment_ids.shape, jnp.int32),
@@ -546,10 +542,10 @@
 def local(token_rows, segment_ids, requests, hot_table, cold_table, input_weight, output_weight, up_weight, down_weight):
     n = lax.axis_size("seq")
     m = lax.axis_size("emb")
-    embedded, gate, q, k, v, info = front(
+    embedded, gate, q, k, v, info, own = front(
         token_rows, segment_ids, jnp.transpose(requests, (0, 2, 1)), hot_table, cold_table, input_weight, n, m
     )
-    attended = attention(info, q, k, v, 8)
+    attended = attention(info, q, k, v, own, 16)
     return finish_layer(attended, gate, embedded, output_weight, up_weight, down_weight, n)[None]
 
 

time: 77.5 us -> 72.4 us (0.934)
  Pallas kernels: 76.1 us -> 70.9 us
    pallas_call x1, Pallas kernels: 17.1 us -> 10.5 us  [attention(): pl.pallas_call(functools.partial(attn_kernel, U), out_shape=jax.ShapeDtyp...]
    pallas_call x1, Pallas kernels: 46.7 us -> 48.4 us  [front(): pl.pallas_call(functools.partial(front_kernel, n, m), out_shape=(jax.Shap...]
where the time goes in v6:
time: 72.4 us; the launch traced here: 71.7 us
  Pallas kernels  70.9 us (98%)
  local copies, waits for them, and re-layouts  0.81 us (1%)
    pallas_call x1, Pallas kernels, front(): pl.pallas_call(functools.partial(front_kernel, n, m), out_shape=(jax.Shap...  48.4 us
    pallas_call x1, Pallas kernels, finish_layer(): pl.pallas_call(functools.partial(finish_kernel, n), out_shape=jax.ShapeDt...  12 us
    pallas_call x1, Pallas kernels, attention(): pl.pallas_call(functools.partial(attn_kernel, U), out_shape=jax.ShapeDtyp...  10.5 us

profile of v6, /device:TPU:0, one launch (start us, length us, event | category | flops | bytes accessed | tf_op | source)
XLA Modules:
  0.0 71.7 jit_solution(10613637701941170959)
XLA Ops:
  0.0 48.4 %front.1 = (bf16[512,512]{1,0:T(8,128)(2,1)S(1)}, bf16[16,32,512]{2,1,0:T(8,128)(2,1)S(1)}, bf16[16,48,512]{2,1,0:T(8,128)(2,1)S(1)}, bf16[8192,48]{1,0:T(8,128)...) custom-call(s32[1,512]{1,0:T(1,128)} %tok_hbm.1, ...), custom_call_target="tpu_custom_call" | custom-call | tf_op jit(solution)/shard_map/front/pallas_call | solution.py:407
  48.4 0.0 copy-start
  48.4 0.0 copy-start.1
  48.4 0.0 copy-start.2
  48.5 10.5 %attn.1.att_ref = bf16[16,32,512]{2,1,0:T(8,128)(2,1)S(1)} custom-call(f32[16,2,512]{2,1,0:T(2,128)S(1)} %get-tuple-element.12.info_ref, bf16[16,48,512]{2,1,0:T(8,128)(2,1)S(1)} %get-tuple-element.13.q_ref, bf16[8192,48]{1,0:T(8,128)(2,1)S(1)} %get-tuple-element.14.k_ref, bf16[16,32,512]{2,1,0:T(8,128)(2,1)S(1)} %get-tuple-element.15.v_ref, ...), custom_call_target="tpu_custom_call" | custom-call | tf_op jit(solution)/shard_map/attn/pallas_call | solution.py:84
  58.9 0.0 copy-done
  58.9 0.0 copy-done.1
  59.0 0.0 copy-done.2
  59.0 12.0 %finish.1 = bf16[512,512]{1,0:T(8,128)(2,1)S(1)} custom-call(bf16[16,32,512]{2,1,0:T(8,128)(2,1)S(1)} %attn.1.att_ref, bf16[16,32,512]{2,1,0:T(8,128)(2,1)S(1)} %get-tuple-element.17.gate_ref, bf16[512,512]{1,0:T(8,128)(2,1)S(1)} %get-tuple-element.18.emb_ref, bf16[512,512]{1,0:T(8,128)(2,1)S(1)} %copy-done.2, bf16[512,2048]{1,0:T(8,128)(2,1)S(1)} %copy-done, ...), custom_call_target="tpu_custom_call" | custom-call | tf_op jit(solution)/shard_map/finish/pallas_call | solution.py:526
  70.9 0.8 %copy.11 = bf16[1,512,512]{2,1,0:T(8,128)(2,1)} copy(bf16[1,512,512]{2,1,0:T(8,128)(2,1)S(1)} %bitcast.2) | data formatting | bytes 1048576
Async XLA Ops:
  48.4 10.5 %copy-start = (bf16[512,2048]{1,0:T(8,128)(2,1)S(1)}, bf16[512,2048]{1,0:T(8,128)(2,1)}, u32[]{:S(2)}) copy-start(bf16[512,2048]{1,0:T(8,128)(2,1)} %up.1) | copy-start | bytes 6291460
  48.4 10.5 %copy-start.1 = (bf16[2048,512]{1,0:T(8,128)(2,1)S(1)}, bf16[2048,512]{1,0:T(8,128)(2,1)}, u32[]{:S(2)}) copy-start(bf16[2048,512]{1,0:T(8,128)(2,1)} %down.1) | copy-start | bytes 6291460
  48.4 10.5 %copy-start.2 = (bf16[512,512]{1,0:T(8,128)(2,1)S(1)}, bf16[512,512]{1,0:T(8,128)(2,1)}, u32[]{:S(2)}) copy-start(bf16[512,512]{1,0:T(8,128)(2,1)} %wo.1) | copy-start | bytes 1572868

commit v7 on v6

--- a/solution.py
+++ b/solution.py
@@ -156,21 +156,31 @@
         dy = lax.rem(2 + 3 * u + 3 * (u // 2) + 2 * (u // 3), side)
         return dz, dy
 
-    def peer_at(dx, core, step):
-        dz, dy = away(step)
-        return (lax.rem(me_x + dx, side) * 2 + core) * n + lax.rem(me_z + dz, side) * side + lax.rem(me_y + dy, side)
-
-    def signal(step, carry):
-        for dx in far:
-            for core in range(2):
-                peer = peer_at(dx, core, step)
-
-                @pl.when(peer != me)
-                def _():
-                    pl.semaphore_signal(barrier, inc=1, device_id=device(peer), device_id_type=MESH)
-        return carry
-
-    lax.fori_loop(0, n, signal, 0)
+    columns = [[lax.rem(me_x + dx, side) * 2 + core for core in range(2)] for dx in range(side)]
+    lanes_y = [lax.rem(me_y + dy, side) for dy in range(side)]
+
+    def to_each(act, offsets):
+        def plane(t, carry):
+            z = lax.rem(me_z + lax.rem(2 + 3 * t + 3 * (t // 2) + 2 * (t // 3), side), side) * side
+            for dy in far:
+                seq = z + lanes_y[dy]
+                for dx in offsets:
+                    for emb in columns[dx]:
+                        if dx == 0 and dy == 0:
+
+                            @pl.when(emb * n + seq != me)
+                            def _():
+                                act(emb, seq)
+                        else:
+                            act(emb, seq)
+            return carry
+
+        lax.fori_loop(0, side, plane, 0)
+
+    def signal(emb, seq):
+        pl.semaphore_signal(barrier, inc=1, device_id={"emb": emb, "seq": seq}, device_id_type=MESH)
+
+    to_each(signal, far)
     hot_load = pltpu.make_async_copy(hot_hbm, hot, lsems.at[0])
     cold_load = pltpu.make_async_copy(cold_hbm, cold, lsems.at[1])
     w_load = pltpu.make_async_copy(w_hbm, w_ref, lsems.at[2])
@@ -201,23 +211,13 @@
     packed[...] = select_exact(unpacker(rank, 0, tokens), jnp.broadcast_to(tok, (128, tokens)).T)
     pl.semaphore_wait(barrier, total - 1)
 
-    def ask(peer, src):
-        return pltpu.make_async_remote_copy(
-            src_ref=asks.at[peer], dst_ref=asked.at[src], send_sem=msems.at[0], recv_sem=msems.at[1],
-            device_id=device(peer), device_id_type=MESH,
-        )
-
-    def start_ask(step, carry):
-        for dx in far:
-            for core in range(2):
-                peer = peer_at(dx, core, step)
-
-                @pl.when(peer != me)
-                def _():
-                    ask(peer, me).start()
-        return carry
-
-    lax.fori_loop(0, n, start_ask, 0)
+    def ask(emb, seq):
+        pltpu.make_async_remote_copy(
+            src_ref=asks.at[emb * n + seq], dst_ref=asked.at[me], send_sem=msems.at[0], recv_sem=msems.at[1],
+            device_id={"emb": emb, "seq": seq}, device_id_type=MESH,
+        ).start()
+
+    to_each(ask, far)
 
     def tell(step, carry):
         pltpu.make_async_remote_copy(
@@ -293,11 +293,11 @@
     idx[...] = jnp.broadcast_to(ids, (slots, 128))
     cold_load.wait()
 
-    def give(peer, src):
-        return pltpu.make_async_remote_copy(
-            src_ref=rows_out.at[peer], dst_ref=rows_in.at[src], send_sem=msems.at[2], recv_sem=msems.at[3],
-            device_id=device(peer), device_id_type=MESH,
-        )
+    def give(emb, seq):
+        pltpu.make_async_remote_copy(
+            src_ref=rows_out.at[emb * n + seq], dst_ref=rows_in.at[me], send_sem=msems.at[2], recv_sem=msems.at[3],
+            device_id={"emb": emb, "seq": seq}, device_id_type=MESH,
+        ).start()
 
     def serve(first, second):
         group = total // side
@@ -310,17 +310,7 @@
             share = gat[c * group * 4:(c + 1) * group * 4, :].astype(bf)
             rows_out[pl.ds(x * group, group)] = share.reshape(group, 4, share.shape[1])
 
-        def start_give(step, inner):
-            for dx in (first, second):
-                for core in range(2):
-                    peer = peer_at(dx, core, step)
-
-                    @pl.when(peer != me)
-                    def _():
-                        give(peer, me).start()
-            return inner
-
-        lax.fori_loop(0, n, start_give, 0)
+        to_each(give, (first, second))
 
     serve(2, 1)
     serve(3, 0)
@@ -362,7 +352,7 @@
 
     causal = lax.broadcasted_iota(jnp.int32, (half, half), 0) <= lax.broadcasted_iota(jnp.int32, (half, half), 1)
 
-    def attend_own(src):
+    def attend_own(src, slot):
         q = q_ref[src]
         v = v_ref[src]
         first = pl.multiple_of(src * tokens, tokens)
@@ -371,23 +361,33 @@
         early = silu_half(jnp.dot(early, q, preferred_element_type=f32))
         late = silu_half(jnp.dot(late, q[:, half:], preferred_element_type=f32))
         zero = jnp.zeros((half, half), bf)
-        weights[0:half, 0:half] = jnp.where(causal, early[:, 0:half], zero)
-        weights[0:half, half:] = early[:, half:]
-        weights[half:, half:] = jnp.where(causal, late, zero)
-        own_ref[src, :, 0:half] = jnp.dot(v[:, 0:half], weights[0:half, 0:half], preferred_element_type=f32)
-        own_ref[src, :, half:] = jnp.dot(v, weights[:, half:], preferred_element_type=f32)
+        weights[slot, 0:half, 0:half] = jnp.where(causal, early[:, 0:half], zero)
+        weights[slot, 0:half, half:] = early[:, half:]
+        weights[slot, half:, half:] = jnp.where(causal, late, zero)
+        own_ref[src, :, 0:half] = jnp.dot(v[:, 0:half], weights[slot, 0:half, 0:half], preferred_element_type=f32)
+        own_ref[src, :, half:] = jnp.dot(v, weights[slot, :, half:], preferred_element_type=f32)
+
+    def source(step):
+        dz, dy = away(step)
+        return lax.rem(me_z + side - dz, side) * side + lax.rem(me_y + side - dy, side)
+
+    def arrive(step, before):
+        now = [source(2 * step + 1), source(2 * step + 2)]
+        for src in now:
+            part_copy(1, src, src).wait_recv()
+        for slot in range(2):
+            attend_own(before[slot], slot)
+        for src in now:
+            unpack_cold(src)
+        return tuple(now)
 
     unpack_cold(me_s)
-
-    def arrive(step, before):
-        dz, dy = away(step)
-        src = lax.rem(me_z + side - dz, side) * side + lax.rem(me_y + side - dy, side)
-        part_copy(1, src, src).wait_recv()
-        attend_own(before)
-        unpack_cold(src)
-        return src
-
-    attend_own(lax.fori_loop(0, n - 1, arrive, me_s))
+    start = source(0)
+    part_copy(1, start, start).wait_recv()
+    unpack_cold(start)
+    last = lax.fori_loop(0, n // 2 - 1, arrive, (me_s, start))
+    for slot in range(2):
+        attend_own(last[slot], slot)
     row_all.wait_send()
     info_all.wait_send()
     hot_all.wait_send()
@@ -418,7 +418,7 @@
         in_specs=[hbm] * 6,
         out_specs=(vm,) * 7,
         scratch_shapes=[
-            pltpu.VMEM((tokens, tokens), bf),
+            pltpu.VMEM((2, tokens, tokens), bf),
             pltpu.VMEM((n, 96, tokens), bf),
             pltpu.VMEM(token_rows.shape, jnp.int32),
             pltpu.VMEM(segment_ids.shape, jnp.int32),

time: 72.4 us -> 71.7 us (level)
    pallas_call x1, Pallas kernels: 48.4 us -> 47.2 us  [front(): pl.pallas_call(functools.partial(front_kernel, n, m), out_shape=(jax.Shap...]
    pallas_call x1, Pallas kernels: 12 us -> 12.8 us  [finish_layer(): pl.pallas_call(functools.partial(finish_kernel, n), out_shape=jax.ShapeDt...]
where the time goes in v7:
time: 71.7 us; the launch traced here: 71.3 us
  Pallas kernels  70.4 us (98%)
  local copies, waits for them, and re-layouts  0.81 us (1%)
    pallas_call x1, Pallas kernels, front(): pl.pallas_call(functools.partial(front_kernel, n, m), out_shape=(jax.Shap...  47.2 us
    pallas_call x1, Pallas kernels, finish_layer(): pl.pallas_call(functools.partial(finish_kernel, n), out_shape=jax.ShapeDt...  12.8 us
    pallas_call x1, Pallas kernels, attention(): pl.pallas_call(functools.partial(attn_kernel, U), out_shape=jax.ShapeDtyp...  10.5 us

profile of v7, /device:TPU:0, one launch (start us, length us, event | category | flops | bytes accessed | tf_op | source)
XLA Modules:
  0.0 71.3 jit_solution(4852097572923896693)
XLA Ops:
  0.0 47.2 %front.1 = (bf16[512,512]{1,0:T(8,128)(2,1)S(1)}, bf16[16,32,512]{2,1,0:T(8,128)(2,1)S(1)}, bf16[16,48,512]{2,1,0:T(8,128)(2,1)S(1)}, bf16[8192,48]{1,0:T(8,128)...) custom-call(s32[1,512]{1,0:T(1,128)} %tok_hbm.1, ...), custom_call_target="tpu_custom_call" | custom-call | tf_op jit(solution)/shard_map/front/pallas_call | solution.py:407
  47.2 0.0 copy-start
  47.2 0.0 copy-start.1
  47.2 0.0 copy-start.2
  47.2 10.5 %attn.1.att_ref = bf16[16,32,512]{2,1,0:T(8,128)(2,1)S(1)} custom-call(f32[16,2,512]{2,1,0:T(2,128)S(1)} %get-tuple-element.12.info_ref, bf16[16,48,512]{2,1,0:T(8,128)(2,1)S(1)} %get-tuple-element.13.q_ref, bf16[8192,48]{1,0:T(8,128)(2,1)S(1)} %get-tuple-element.14.k_ref, bf16[16,32,512]{2,1,0:T(8,128)(2,1)S(1)} %get-tuple-element.15.v_ref, ...), custom_call_target="tpu_custom_call" | custom-call | tf_op jit(solution)/shard_map/attn/pallas_call | solution.py:84
  57.7 0.0 copy-done
  57.7 0.0 copy-done.1
  57.7 0.0 copy-done.2
  57.7 12.8 %finish.1 = bf16[512,512]{1,0:T(8,128)(2,1)S(1)} custom-call(bf16[16,32,512]{2,1,0:T(8,128)(2,1)S(1)} %attn.1.att_ref, bf16[16,32,512]{2,1,0:T(8,128)(2,1)S(1)} %get-tuple-element.17.gate_ref, bf16[512,512]{1,0:T(8,128)(2,1)S(1)} %get-tuple-element.18.emb_ref, bf16[512,512]{1,0:T(8,128)(2,1)S(1)} %copy-done.2, bf16[512,2048]{1,0:T(8,128)(2,1)S(1)} %copy-done, ...), custom_call_target="tpu_custom_call" | custom-call | tf_op jit(solution)/shard_map/finish/pallas_call | solution.py:526
  70.5 0.8 %copy.11 = bf16[1,512,512]{2,1,0:T(8,128)(2,1)} copy(bf16[1,512,512]{2,1,0:T(8,128)(2,1)S(1)} %bitcast.2) | data formatting | bytes 1048576
Async XLA Ops:
  47.2 10.5 %copy-start = (bf16[512,2048]{1,0:T(8,128)(2,1)S(1)}, bf16[512,2048]{1,0:T(8,128)(2,1)}, u32[]{:S(2)}) copy-start(bf16[512,2048]{1,0:T(8,128)(2,1)} %up.1) | copy-start | bytes 6291460
  47.2 10.5 %copy-start.1 = (bf16[2048,512]{1,0:T(8,128)(2,1)S(1)}, bf16[2048,512]{1,0:T(8,128)(2,1)}, u32[]{:S(2)}) copy-start(bf16[2048,512]{1,0:T(8,128)(2,1)} %down.1) | copy-start | bytes 6291460
  47.2 10.5 %copy-start.2 = (bf16[512,512]{1,0:T(8,128)(2,1)S(1)}, bf16[512,512]{1,0:T(8,128)(2,1)}, u32[]{:S(2)}) copy-start(bf16[512,512]{1,0:T(8,128)(2,1)} %wo.1) | copy-start | bytes 1572868

commit v8 on v7

--- a/solution.py
+++ b/solution.py
@@ -467,7 +467,7 @@
     greet(n)
 
     tokens = emb_ref.shape[0]
-    rows = tokens // 2
+    rows = tokens // 4
 
     def copy_to(part, peer):
         return pltpu.make_async_remote_copy(
@@ -477,12 +477,12 @@
 
     side = 4
     far = (2, 1, 3, 0)
-    for part in range(2):
+    for part in range(4):
         for dz in far:
             for dy in far:
                 if (dz, dy) != (0, 0):
                     copy_to(part, lax.rem(me // side + dz, side) * side + lax.rem(me + dy, side)).start()
-    for part in range(2):
+    for part in range(4):
         back[part, me] = att_ref[me, :, part * rows:(part + 1) * rows]
 
     def open_one(step, carry):
@@ -511,7 +511,7 @@
         out = hidden + jnp.dot(active, down[...], preferred_element_type=jnp.float32)
         out_ref[span, :] = out.astype(jnp.bfloat16)
 
-    for step in range(2):
+    for step in range(4):
         tail(step)
     pltpu.make_async_remote_copy(
         src_ref=att_ref.at[every], dst_ref=att_ref.at[every], send_sem=sends, recv_sem=recvs.at[0],
@@ -529,10 +529,10 @@
         in_specs=[vm] * 6,
         out_specs=vm,
         scratch_shapes=[
-            pltpu.VMEM((2, n, 32, tokens // 2), bf),
+            pltpu.VMEM((4, n, 32, tokens // 4), bf),
             pltpu.VMEM((n, 32, tokens), jnp.float32),
             pltpu.SemaphoreType.DMA,
-            pltpu.SemaphoreType.DMA((2,)),
+            pltpu.SemaphoreType.DMA((4,)),
         ],
         compiler_params=pltpu.CompilerParams(collective_id=2, has_side_effects=True, vmem_limit_bytes=20 << 20),
         name="finish",

time: 71.7 us -> 71.3 us (level)
  no operation moved by 1% of the time
where the time goes in v8:
time: 71.3 us; the launch traced here: 70.9 us
  Pallas kernels  70 us (98%)
  local copies, waits for them, and re-layouts  0.81 us (1%)
    pallas_call x1, Pallas kernels, front(): pl.pallas_call(functools.partial(front_kernel, n, m), out_shape=(jax.Shap...  47.2 us
    pallas_call x1, Pallas kernels, finish_layer(): pl.pallas_call(functools.partial(finish_kernel, n), out_shape=jax.ShapeDt...  12.4 us
    pallas_call x1, Pallas kernels, attention(): pl.pallas_call(functools.partial(attn_kernel, U), out_shape=jax.ShapeDtyp...  10.5 us

profile of v8, /device:TPU:0, one launch (start us, length us, event | category | flops | bytes accessed | tf_op | source)
XLA Modules:
  0.0 70.9 jit_solution(14197344793491411284)
XLA Ops:
  0.0 47.2 %front.1 = (bf16[512,512]{1,0:T(8,128)(2,1)S(1)}, bf16[16,32,512]{2,1,0:T(8,128)(2,1)S(1)}, bf16[16,48,512]{2,1,0:T(8,128)(2,1)S(1)}, bf16[8192,48]{1,0:T(8,128)...) custom-call(s32[1,512]{1,0:T(1,128)} %tok_hbm.1, ...), custom_call_target="tpu_custom_call" | custom-call | tf_op jit(solution)/shard_map/front/pallas_call | solution.py:407
  47.2 0.0 copy-start
  47.2 0.0 copy-start.1
  47.2 0.0 copy-start.2
  47.2 10.5 %attn.1.att_ref = bf16[16,32,512]{2,1,0:T(8,128)(2,1)S(1)} custom-call(f32[16,2,512]{2,1,0:T(2,128)S(1)} %get-tuple-element.12.info_ref, bf16[16,48,512]{2,1,0:T(8,128)(2,1)S(1)} %get-tuple-element.13.q_ref, bf16[8192,48]{1,0:T(8,128)(2,1)S(1)} %get-tuple-element.14.k_ref, bf16[16,32,512]{2,1,0:T(8,128)(2,1)S(1)} %get-tuple-element.15.v_ref, ...), custom_call_target="tpu_custom_call" | custom-call | tf_op jit(solution)/shard_map/attn/pallas_call | solution.py:84
  57.7 0.0 copy-done
  57.7 0.0 copy-done.1
  57.7 0.0 copy-done.2
  57.7 12.4 %finish.1 = bf16[512,512]{1,0:T(8,128)(2,1)S(1)} custom-call(bf16[16,32,512]{2,1,0:T(8,128)(2,1)S(1)} %attn.1.att_ref, bf16[16,32,512]{2,1,0:T(8,128)(2,1)S(1)} %get-tuple-element.17.gate_ref, bf16[512,512]{1,0:T(8,128)(2,1)S(1)} %get-tuple-element.18.emb_ref, bf16[512,512]{1,0:T(8,128)(2,1)S(1)} %copy-done.2, bf16[512,2048]{1,0:T(8,128)(2,1)S(1)} %copy-done, ...), custom_call_target="tpu_custom_call" | custom-call | tf_op jit(solution)/shard_map/finish/pallas_call | solution.py:526
  70.1 0.8 %copy.11 = bf16[1,512,512]{2,1,0:T(8,128)(2,1)} copy(bf16[1,512,512]{2,1,0:T(8,128)(2,1)S(1)} %bitcast.2) | data formatting | bytes 1048576
Async XLA Ops:
  47.2 10.5 %copy-start = (bf16[512,2048]{1,0:T(8,128)(2,1)S(1)}, bf16[512,2048]{1,0:T(8,128)(2,1)}, u32[]{:S(2)}) copy-start(bf16[512,2048]{1,0:T(8,128)(2,1)} %up.1) | copy-start | bytes 6291460
  47.2 10.5 %copy-start.1 = (bf16[2048,512]{1,0:T(8,128)(2,1)S(1)}, bf16[2048,512]{1,0:T(8,128)(2,1)}, u32[]{:S(2)}) copy-start(bf16[2048,512]{1,0:T(8,128)(2,1)} %down.1) | copy-start | bytes 6291460
  47.2 10.5 %copy-start.2 = (bf16[512,512]{1,0:T(8,128)(2,1)S(1)}, bf16[512,512]{1,0:T(8,128)(2,1)}, u32[]{:S(2)}) copy-start(bf16[512,512]{1,0:T(8,128)(2,1)} %wo.1) | copy-start | bytes 1572868
